TPU v7x, 32 devices: a whole 2x2x4 slice. The times are simulated.
32 devices in a mesh: atom: 16 (over z, y, core), band: 2 (over x).
Axes of the slice: x: 2, y: 2, z: 4, core: 2. Of those that a mesh axis runs over, the one named last changes fastest.
Arguments:
- wave_rows: bfloat16 [256, 65536], P('atom', 'band'), may hold values from -6 to 6
- projectors: bfloat16 [2048, 65536], P('atom', 'band'), may hold values from -0.0234375 to 0.0234375
- dij_table: float32 [16, 8, 8], replicated, may hold values from -6 to 6
- dij_index: int32 [256], P('atom'), may hold values from 0 to 15
- proj_count: int32 [256], P('atom'), may hold values from 1 to 8
Outputs:
- nonlocal_rows: bfloat16 [256, 65536], P('atom', 'band')
All inputs are finite; a program needn't handle non-finite values.
Results may differ from a plain program's by a relative error of at most 0.0049.
Values may be sent and summed in bfloat16 or wider, within the bound.
A program may use at most 128 MiB of HBM per device.

v0:
```python
import functools

import jax
import jax.numpy as jnp
from jax import lax
from jax.experimental import pallas as pl
from jax.experimental.pallas import tpu as pltpu
from jax.sharding import PartitionSpec as P

MESH = pl.DeviceIdType.MESH


def mix_matrix(table, index, count):
    atoms = index.shape[0]
    kinds, per_atom = table.shape[:2]
    depth = atoms * per_atom
    exact = functools.partial(
        lax.dot_general, precision=lax.Precision.HIGHEST, preferred_element_type=jnp.float32)

    def iota(shape, axis):
        return lax.broadcasted_iota(jnp.int32, shape, axis)

    row, lane = iota((depth, depth), 0), iota((depth, depth), 1)
    spread = (iota((depth, atoms), 0) // per_atom == iota((depth, atoms), 1)).astype(jnp.float32)
    pick = (lax.rem(iota((depth, per_atom), 0), per_atom) == iota((depth, per_atom), 1)).astype(
        jnp.float32)
    plain = (((1,), (0,)), ((), ()))

    def over_rows(value):
        value = jnp.broadcast_to(value.astype(jnp.float32), (atoms, depth))
        return exact(spread, value, plain)

    kind, active = over_rows(index), over_rows(count)
    chosen = jnp.zeros((depth, depth), jnp.float32)
    for k in range(kinds):
        turned = exact(pick, table[k], (((1,), (1,)), ((), ())))
        wide = exact(turned, pick, (((1,), (1,)), ((), ())))
        chosen = jnp.where(jnp.abs(kind - k) < 0.5, wide, chosen)
    inside = lax.rem(row, per_atom).astype(jnp.float32) < active - 0.5
    inside &= lax.rem(lane, per_atom).astype(jnp.float32) < active - 0.5
    inside &= row // per_atom == lane // per_atom
    return jnp.where(inside, chosen, 0.0)


def kernel(chips, bands, wave, proj, table, index, count, out, gath, full, ring, term, inter, swap,
           parts, mixes, weights, local_sem, wave_sem, proj_sem, mix_sem, gs_sem, gr_sem,
           rs_sem, rr_sem, swap_sem, part_s, part_r, wt_sem, out_sem, out_local):
    atom = lax.axis_index("atom")
    band = lax.axis_index("band")
    core = lax.rem(atom, 2)
    other = 1 - core
    chip = atom // 2
    odd = lax.rem(chip, 2)
    pos = odd * (chips - 1 - chip // 2) + (1 - odd) * (chip // 2)

    def device(place):
        place = lax.rem(place + 2 * chips, chips)
        far = place // (chips // 2)
        number = far * (2 * (chips - 1 - place) + 1) + (1 - far) * 2 * place
        return (number * 2 + core, band)

    peer = (chip * 2 + other, band)
    ahead, behind = device(pos + 1), device(pos - 1)
    partners = [(atom, lax.rem(band + k, bands)) for k in range(1, bands)]
    toward = (ahead, behind)
    sign = (1, -1)

    rows = wave.shape[0]
    depth = proj.shape[0]
    wide = full.shape[2]
    part_wide = wide // 2
    half_rows = inter.shape[1] // 2
    steps = chips - 1

    barrier = pltpu.get_barrier_semaphore()
    for target in [peer, ahead, behind] + partners:
        pl.semaphore_signal(barrier, inc=1, device_id=target, device_id_type=MESH)
    pl.semaphore_wait(barrier, 3 + len(partners))

    def col(which, d):
        return pl.ds(pl.multiple_of((2 * which + d) * wide, wide), wide)

    def block(place):
        place = lax.rem(place + 2 * chips, chips)
        return pl.ds(pl.multiple_of(place * rows, rows), rows)

    def remote(src, dst, s_sem, r_sem, target):
        return pltpu.make_async_remote_copy(
            src_ref=src, dst_ref=dst, send_sem=s_sem, recv_sem=r_sem,
            device_id=target, device_id_type=MESH)

    own_copies, peer_out, peer_in = [], [], []
    for d in range(2):
        c = remote(wave.at[:, col(other, d)], gath.at[d, core, block(pos), :],
                   wave_sem.at[0, d], wave_sem.at[1, d], peer)
        c.start()
        peer_out.append(c)
        c = pltpu.make_async_copy(wave.at[:, col(core, d)], gath.at[d, core, block(pos), :],
                                  local_sem.at[d])
        c.start()
        own_copies.append(c)
        peer_in.append(remote(wave.at[:, col(other, d)], gath.at[d, other, block(pos), :],
                              wave_sem.at[0, d], wave_sem.at[1, d], peer))

    def hop(d, place, r, s, h):
        piece = gath.at[d, r, block(place), pl.ds(h * part_wide, part_wide)]
        return remote(piece, piece, gs_sem.at[d, s, r, h], gr_sem.at[d, s, r, h], toward[d])

    def gather(d, s, r, h):
        return hop(d, pos - sign[d] * s, r, s, h)

    def gathered(d, s, r, h):
        return hop(d, pos - sign[d] * (s + 1), r, s, h)

    def gather_first(r):
        for h in range(2):
            for d in range(2):
                gather(d, 0, r, h).start()

    def gather_half(r, s, h, final=False):
        for d in range(2):
            gathered(d, s, r, h).wait_recv()
            if not final:
                gather(d, s + 1, r, h).start()

    def gather_step(r, s, final=False):
        for h in range(2):
            gather_half(r, s, h, final)

    for d in range(2):
        own_copies[d].wait()
        peer_in[d].wait_recv()
        for h in range(2):
            gather(d, 0, 0, h).start()

    here = pl.ds(pl.multiple_of(core * depth, depth), depth)
    there = pl.ds(pl.multiple_of(other * depth, depth), depth)
    proj_local, proj_out = [], []
    for d in range(2):
        c = pltpu.make_async_copy(proj.at[:, col(core, d)], full.at[d, here, :], local_sem.at[2 + d])
        c.start()
        proj_local.append(c)
        c = remote(proj.at[:, col(other, d)], full.at[d, here, :], proj_sem.at[0, d],
                   proj_sem.at[1, d], peer)
        c.start()
        proj_out.append(c)
    mixes[core] = mix_matrix(table, index[...], count[...])
    mix_out = remote(mixes.at[core], mixes.at[core], mix_sem.at[0], mix_sem.at[1], peer)
    mix_out.start()
    mix_in = remote(mixes.at[other], mixes.at[other], mix_sem.at[0], mix_sem.at[1], peer)

    kt = min(1024, wide)
    nt = min(512, wide)
    keep = pl.ds(pl.multiple_of(core * half_rows, half_rows), half_rows)
    give = pl.ds(pl.multiple_of(other * half_rows, half_rows), half_rows)

    def meet(r, d):
        def body(t, acc):
            cols = pl.ds(pl.multiple_of(t * kt, kt), kt)
            return acc + lax.dot_general(
                gath[d, r, :, cols], full[d, :, cols], (((1,), (1,)), ((), ())),
                preferred_element_type=jnp.float32)

        start = inter[r] if d else jnp.zeros(inter.shape[1:], jnp.float32)
        inter[r] = lax.fori_loop(0, wide // kt, body, start)

    def core_sum(r):
        return remote(inter.at[r, give, :], swap.at[r], swap_sem.at[0, r], swap_sem.at[1, r], peer)

    def band_sum(r, k):
        return remote(inter.at[r, keep, :], parts.at[r, k], part_s.at[r, k], part_r.at[r, k],
                      partners[k])

    def share(r, which):
        piece = weights.at[r, which, :]
        return remote(piece, piece, wt_sem.at[0, r], wt_sem.at[1, r], peer)

    def middle_two(r):
        core_sum(r).wait()
        inter[r, keep, :] = inter[r, keep, :] + swap[r]
        for k in range(len(partners)):
            band_sum(r, k).start()

    def middle_three(r):
        value = inter[r, keep, :]
        for k in range(len(partners)):
            band_sum(r, k).wait()
            value = value + parts[r, k]
        for m in range(2):
            cut = slice(m * depth, (m + 1) * depth)
            weights[r, keep, cut] = lax.dot_general(
                value[:, cut], mixes[m], (((1,), (0,)), ((), ())),
                precision=lax.Precision.HIGHEST,
                preferred_element_type=jnp.float32).astype(weights.dtype)
        share(r, keep).start()

    def apply(r, d):
        @pl.loop(0, wide // nt)
        def _(t):
            cols = pl.ds(pl.multiple_of(t * nt, nt), nt)
            term[r, d, :, cols] = jnp.dot(
                weights[r], full[d, :, cols], preferred_element_type=jnp.float32)

    def fold(d, s, r, h, arrived):
        where = block(pos - sign[d] * (s + 1))

        @pl.loop(0, part_wide // nt)
        def _(t):
            cols = pl.ds(pl.multiple_of(h * part_wide + t * nt, nt), nt)
            new = term[r, d, where, cols]
            if arrived:
                new = new + ring[d, r, s, :, cols].astype(jnp.float32)
            ring[d, r, s, :, cols] = new.astype(ring.dtype)

    def scatter(d, s, r, h):
        cols = pl.ds(h * part_wide, part_wide)
        return remote(ring.at[d, r, s, :, cols], ring.at[d, r, s + 1, :, cols],
                      rs_sem.at[d, s, r, h], rr_sem.at[d, s, r, h], toward[d])

    def scatter_first(r, d):
        apply(r, d)
        for h in range(2):
            fold(d, 0, r, h, False)
            scatter(d, 0, r, h).start()

    def scatter_half(r, s, h, final=False):
        for d in range(2):
            scatter(d, s, r, h).wait_recv()
            fold(d, s + 1, r, h, True)
            if not final:
                scatter(d, s + 1, r, h).start()

    def scatter_step(r, s, final=False):
        for h in range(2):
            scatter_half(r, s, h, final)

    lag = min(3, steps - 1)
    tail = min(2, steps - 1)

    @pl.loop(0, lag)
    def _(s):
        gather_step(0, s)

    gather_first(1)

    @pl.loop(0, steps - 1 - lag)
    def _(s):
        gather_step(0, s + lag)
        gather_step(1, s)

    for d in range(2):
        proj_local[d].wait()
        remote(proj.at[:, col(other, d)], full.at[d, there, :], proj_sem.at[0, d],
               proj_sem.at[1, d], peer).wait_recv()
    mix_in.wait_recv()

    gather_step(0, steps - 1, True)
    gather_step(1, steps - 1 - lag)
    halves = [(t, h) for t in range(steps - lag, steps - 1) for h in range(2)]

    def pass_on(count):
        for t, h in halves[:count]:
            gather_half(1, t, h)
        del halves[:count]

    meet(0, 0)
    pass_on(1)
    meet(0, 1)
    core_sum(0).start()
    pass_on(1)
    middle_two(0)
    pass_on(len(halves))
    middle_three(0)
    share(0, give).wait_recv()
    scatter_first(0, 0)
    scatter_first(0, 1)
    gather_step(1, steps - 1, True)
    meet(1, 0)
    scatter_half(0, 0, 0)
    meet(1, 1)
    core_sum(1).start()
    scatter_half(0, 0, 1)
    middle_two(1)
    for s in range(1, tail):
        scatter_step(0, s)
    middle_three(1)
    share(1, give).wait_recv()
    scatter_first(1, 0)
    scatter_first(1, 1)

    @pl.loop(0, steps - 1 - tail)
    def _(s):
        scatter_step(0, s + tail)
        scatter_step(1, s)

    scatter_step(0, steps - 1, True)

    @pl.loop(steps - 1 - tail, steps - 1)
    def _(s):
        scatter_step(1, s)

    scatter_step(1, steps - 1, True)

    last = []
    for d in range(2):
        c = remote(ring.at[d, other, steps], out.at[:, col(core, d)], out_sem.at[0, d],
                   out_sem.at[1, d], peer)
        c.start()
        o = pltpu.make_async_copy(ring.at[d, core, steps], out.at[:, col(core, d)],
                                  out_local.at[d])
        o.start()
        last.append((c, o))

    for d in range(2):
        peer_out[d].wait_send()
        proj_out[d].wait_send()
    mix_out.wait_send()
    for r in range(2):
        share(r, keep).wait_send()

    @pl.loop(0, steps)
    def _(s):
        for d in range(2):
            for r in range(2):
                for h in range(2):
                    gather(d, s, r, h).wait_send()
                    scatter(d, s, r, h).wait_send()

    for d in range(2):
        last[d][0].wait_send()
        remote(ring.at[d, core, steps], out.at[:, col(other, d)],
               out_sem.at[0, d], out_sem.at[1, d], peer).wait_recv()
        last[d][1].wait()


def shards(chips, bands, wave_rows, projectors, dij_table, dij_index, proj_count):
    atom_local = dij_index.shape[0]
    depth = atom_local * dij_table.shape[1]
    rows, columns = wave_rows.shape
    wide = columns // 4
    both = 2 * depth
    steps = chips - 1
    others = max(bands - 1, 1)
    dma = pltpu.SemaphoreType.DMA
    f32, bf16 = jnp.float32, jnp.bfloat16
    anywhere = pl.BlockSpec(memory_space=pl.ANY)
    return pl.pallas_call(
        functools.partial(kernel, chips, bands),
        out_shape=jax.ShapeDtypeStruct((rows, columns), bf16),
        in_specs=[anywhere, anywhere] + [pl.BlockSpec(memory_space=pltpu.VMEM)] * 3,
        out_specs=anywhere,
        scratch_shapes=[
            pltpu.VMEM((2, 2, chips * rows, wide), bf16),
            pltpu.VMEM((2, both, wide), bf16),
            pltpu.VMEM((2, 2, chips, rows, wide), bf16),
            pltpu.VMEM((2, 2, chips * rows, wide), f32),
            pltpu.VMEM((2, chips * rows, both), f32),
            pltpu.VMEM((2, chips * rows // 2, both), f32),
            pltpu.VMEM((2, others, chips * rows // 2, both), f32),
            pltpu.VMEM((2, depth, depth), f32),
            pltpu.VMEM((2, chips * rows, both), bf16),
            dma((4,)), dma((2, 2)), dma((2, 2)), dma((2,)),
            dma((2, steps, 2, 2)), dma((2, steps, 2, 2)),
            dma((2, steps, 2, 2)), dma((2, steps, 2, 2)),
            dma((2, 2)), dma((2, others)), dma((2, others)),
            dma((2, 2)), dma((2, 2)), dma((2,)),
        ],
        compiler_params=pltpu.CompilerParams(
            collective_id=0, has_side_effects=True, vmem_limit_bytes=60 * 1024 * 1024
        ),
    )(wave_rows, projectors, dij_table, dij_index[:, None], proj_count[:, None])


def solution(mesh):
    in_specs = (P("atom", "band"), P("atom", "band"), P(), P("atom"), P("atom"))
    chips = mesh.shape["atom"] // 2
    bands = mesh.shape["band"]
    return jax.jit(
        jax.shard_map(
            functools.partial(shards, chips, bands),
            mesh=mesh,
            in_specs=in_specs,
            out_specs=P("atom", "band"),
            check_vma=False,
        )
    )
```

profile of v0, /device:TPU:0, one launch (start us, length us, event | category | flops | bytes accessed | tf_op | source)
XLA Modules:
  0.0 185.1 jit_solution(430617013446247252)
XLA Ops:
  0.0 1.3 copy.7.index
  1.3 1.3 copy.8.count
  2.6 1.5 copy.6.table
  4.1 178.7 %shard_map.68 = bf16[16,32768]{1,0:T(8,128)(2,1)} custom-call(bf16[16,32768]{1,0:T(8,128)(2,1)} %wave.1, bf16[128,32768]{1,0:T(8,128)(2,1)} %proj.1, f32[16,8,8]{2,1,0:T(8,128)} %copy.6.table, s32[16,1]{1,0:T(8,128)} %copy.7.index, s32[16,1]{1,0:T(8,128)} %copy.8.count), custom_call_target="tpu_custom_call" | custom-call | tf_op jit(solution)/jit(shards)/shard_map/pallas_call | solution.py:347
  182.9 2.3 %copy.10 = bf16[16,32768]{1,0:T(8,128)(2,1)} copy(bf16[16,32768]{1,0:T(8,128)(2,1)} %shard_map.68) | data formatting | bytes 2097152
where the time goes:
time: 185 us
  Pallas kernels  179 us (97%)
  local copies, waits for them, and re-layouts  6.38 us (3%)
    pallas_call x1, Pallas kernels, shards(): pl.pallas_call(functools.partial(kernel, chips, bands), out_shape=jax.Sha...  179 us
    unnamed x2, local copies, waits for them, and re-layouts  3.73 us

commit v1 on v0

v1 whole, which is shorter than its diff:
```python
import functools

import jax
import jax.numpy as jnp
from jax import lax
from jax.experimental import pallas as pl
from jax.experimental.pallas import tpu as pltpu
from jax.sharding import PartitionSpec as P

MESH = pl.DeviceIdType.MESH
GROUPS = 2
GATHER_SHARE = (0.8125, 0.5)
SCATTER_SHARE = (0.5, 0.8125)


def mix_matrix(table, index, count):
    atoms = index.shape[0]
    kinds, per_atom = table.shape[:2]
    depth = atoms * per_atom
    exact = functools.partial(
        lax.dot_general, precision=lax.Precision.HIGHEST, preferred_element_type=jnp.float32)

    def iota(shape, axis):
        return lax.broadcasted_iota(jnp.int32, shape, axis)

    row, lane = iota((depth, depth), 0), iota((depth, depth), 1)
    spread = (iota((depth, atoms), 0) // per_atom == iota((depth, atoms), 1)).astype(jnp.float32)
    pick = (lax.rem(iota((depth, per_atom), 0), per_atom) == iota((depth, per_atom), 1)).astype(
        jnp.float32)
    plain = (((1,), (0,)), ((), ()))

    def over_rows(value):
        value = jnp.broadcast_to(value.astype(jnp.float32), (atoms, depth))
        return exact(spread, value, plain)

    kind, active = over_rows(index), over_rows(count)
    chosen = jnp.zeros((depth, depth), jnp.float32)
    for k in range(kinds):
        turned = exact(pick, table[k], (((1,), (1,)), ((), ())))
        wide = exact(turned, pick, (((1,), (1,)), ((), ())))
        chosen = jnp.where(jnp.abs(kind - k) < 0.5, wide, chosen)
    inside = lax.rem(row, per_atom).astype(jnp.float32) < active - 0.5
    inside &= lax.rem(lane, per_atom).astype(jnp.float32) < active - 0.5
    inside &= row // per_atom == lane // per_atom
    return jnp.where(inside, chosen, 0.0)


def chunks_of(width, share):
    unit = max(width // 32, 128)
    units = width // unit
    single = min(max(round(share * units), 1), units)
    first = (single + 1) // 2
    cuts = [(0, first, True), (first, single - first, True), (single, units - single, False)]
    return [(start * unit, size * unit, kind) for start, size, kind in cuts if size]


def flows_of(chunks):
    return ([(c, 0) for c, chunk in enumerate(chunks) if chunk[2]]
            + [(c, lane) for c, chunk in enumerate(chunks) if not chunk[2] for lane in range(2)])


def kernel(length, bands, gather_plan, scatter_plan, wave, proj, table, index, count, out, gath,
           full, term, ysend, yrecv, slot, inter, swap, parts, mixes, weights, own_sem, wave_sem,
           proj_sem, mix_sem, az_s, az_r, ay_s, ay_r, rz_s, rz_r, ry_s, ry_r, swap_sem, part_s,
           part_r, wt_sem, out_sem, out_local):
    atom = lax.axis_index("atom")
    band = lax.axis_index("band")
    core = lax.rem(atom, 2)
    other = 1 - core
    y = lax.rem(atom // 2, 2)
    z = atom // 4

    groups, _, _, rows, width = gath.shape
    depth = proj.shape[0]
    both = 2 * depth
    half_rows = length * rows
    unit = max(width // 32, 128)

    def device(lane, place, side):
        return ((place * 2 + lane) * 2 + side, band)

    peer = device(y, z, other)
    across = device(1 - y, z, core)
    toward = (device(y, z + 1, core), device(y, z - 1, core))
    can = (z < length - 1, z > 0)
    edge = (z == 0, z == length - 1)
    partners = [(atom, lax.rem(band + k, bands)) for k in range(1, bands)]

    barrier = pltpu.get_barrier_semaphore()
    for target in [peer, across] + partners:
        pl.semaphore_signal(barrier, inc=1, device_id=target, device_id_type=MESH)
    for d in range(2):
        @pl.when(can[d])
        def _():
            pl.semaphore_signal(barrier, inc=1, device_id=toward[d], device_id_type=MESH)
    pl.semaphore_wait(
        barrier, 2 + len(partners) + can[0].astype(jnp.int32) + can[1].astype(jnp.int32))

    def remote(src, dst, s_sem, r_sem, target):
        return pltpu.make_async_remote_copy(
            src_ref=src, dst_ref=dst, send_sem=s_sem, recv_sem=r_sem,
            device_id=target, device_id_type=MESH)

    def span(side, start, size):
        return pl.ds(pl.multiple_of(side * width + start, 128), size)

    own_copies, peer_out, peer_in = [], [], []
    for sub in range(groups // 2):
        here = pl.ds(sub * rows, rows)
        c = remote(wave.at[here, span(other, 0, width)], gath.at[2 * sub + core, 0, z],
                   wave_sem.at[0, sub], wave_sem.at[1, sub], peer)
        c.start()
        peer_out.append(c)
        c = pltpu.make_async_copy(wave.at[here, span(core, 0, width)],
                                  gath.at[2 * sub + core, 0, z], own_sem.at[sub])
        c.start()
        own_copies.append(c)
        peer_in.append(remote(wave.at[here, span(other, 0, width)],
                              gath.at[2 * sub + other, 0, z],
                              wave_sem.at[0, sub], wave_sem.at[1, sub], peer))

    gather_flows = [flows_of(p) for p in gather_plan]
    scatter_flows = [flows_of(p) for p in scatter_plan]

    def singles(plan):
        return [c for c, chunk in enumerate(plan) if chunk[2]]

    def doubles(plan):
        return [c for c, chunk in enumerate(plan) if not chunk[2]]

    def cols(chunk):
        return pl.ds(chunk[0], chunk[1])

    def a_z(g, f, block, d, own=False):
        c, lane = gather_flows[g][f]
        piece = gath.at[g, lane, block, :, cols(gather_plan[g][c])]
        sent = length if own and d else block
        return remote(piece, piece, az_s.at[g, f, sent], az_r.at[g, f, block], toward[d])

    def a_y(g, c, block):
        where = cols(gather_plan[g][c])
        return remote(gath.at[g, 0, block, :, where], gath.at[g, 1, block, :, where],
                      ay_s.at[g, c, block], ay_r.at[g, c, block], across)

    def own_z(g, d, when, single, lane=0):
        for f, (c, on) in enumerate(gather_flows[g]):
            if gather_plan[g][c][2] == single and on == lane:
                @pl.when(when)
                def _():
                    a_z(g, f, z, d, True).start()

    def own_y(g, single):
        for c in (singles if single else doubles)(gather_plan[g]):
            a_y(g, c, z).start()

    def arrive(g, f, delta):
        c, _ = gather_flows[g][f]
        for d in range(2):
            block = z - delta if d == 0 else z + delta

            @pl.when(block >= 0 if d == 0 else block < length)
            def _():
                copy = a_z(g, f, block, d)
                copy.wait_recv()

                @pl.when(can[d])
                def _():
                    copy.start()
                if gather_plan[g][c][2]:
                    a_y(g, c, block).start()

    def gather_early(g):
        for d in range(2):
            own_z(g, d, can[d] & edge[d], True)

    def gather_open(g, early):
        own_y(g, False)
        for d in range(2):
            own_z(g, d, can[d] & jnp.logical_not(edge[d]) if early else can[d], True)
        own_y(g, True)

    def gather_step(g, delta):
        for f, (c, _) in enumerate(gather_flows[g]):
            if gather_plan[g][c][2]:
                arrive(g, f, delta)
        if delta == 1:
            for d in range(2):
                own_z(g, d, can[d], False)
            for c in doubles(gather_plan[g]):
                a_y(g, c, z).wait_recv()
            for d in range(2):
                own_z(g, d, can[d], False, 1)

    def gather_double(g, delta):
        for f, (c, _) in enumerate(gather_flows[g]):
            if not gather_plan[g][c][2]:
                arrive(g, f, delta)

    def gather_close(g):
        for c in singles(gather_plan[g]):
            for block in range(length):
                a_y(g, c, block).wait_recv()

    kt = min(1024, width)
    keep, give = core, other

    def meet(g):
        def body(t, acc):
            where = pl.ds(pl.multiple_of(t * kt, kt), kt)
            left = gath[g, :, :, :, where].reshape(2 * half_rows, kt)
            return acc + lax.dot_general(left, full[:, where], (((1,), (1,)), ((), ())),
                                         preferred_element_type=jnp.float32)

        total = lax.fori_loop(0, width // kt, body, jnp.zeros((2 * half_rows, both), jnp.float32))
        inter[g] = total.reshape(2, half_rows, both)

    def core_sum(g):
        return remote(inter.at[g, give], swap.at[g], swap_sem.at[0, g], swap_sem.at[1, g], peer)

    def band_sum(g, k):
        return remote(inter.at[g, keep], parts.at[g, k], part_s.at[g, k], part_r.at[g, k],
                      partners[k])

    def share(g, which):
        piece = weights.at[g, which]
        return remote(piece, piece, wt_sem.at[0, g], wt_sem.at[1, g], peer)

    def middle_two(g):
        core_sum(g).wait()
        inter[g, keep] = inter[g, keep] + swap[g]
        for k in range(len(partners)):
            band_sum(g, k).start()

    def middle_three(g):
        value = inter[g, keep]
        for k in range(len(partners)):
            band_sum(g, k).wait()
            value = value + parts[g, k]
        for m in range(2):
            cut = slice(m * depth, (m + 1) * depth)
            weights[g, keep, :, cut] = lax.dot_general(
                value[:, cut], mixes[m], (((1,), (0,)), ((), ())),
                precision=lax.Precision.HIGHEST,
                preferred_element_type=jnp.float32).astype(weights.dtype)
        share(g, keep).start()

    def r_y(g, c, block):
        where = cols(scatter_plan[g][c])
        return remote(ysend.at[g, block, :, where], yrecv.at[g, block, :, where],
                      ry_s.at[g, c, block], ry_r.at[g, c, block], across)

    def r_z(g, f, block, d, last):
        c, lane = scatter_flows[g][f]
        where = cols(scatter_plan[g][c])
        lands = length if last and d else block
        return remote(slot.at[g, lane, block, :, where], slot.at[g, lane, lands, :, where],
                      rz_s.at[g, f, block], rz_r.at[g, f, lands], toward[d])

    def tiles(chunk, body):
        start, size, _ = chunk

        @pl.loop(0, size // unit)
        def _(t):
            body(pl.ds(pl.multiple_of(start + t * unit, unit), unit))

    def apply(g, c):
        chunk = scatter_plan[g][c]

        def body(where):
            new = jnp.dot(weights[g].reshape(2 * half_rows, both), full[:, where],
                          preferred_element_type=jnp.float32)
            if chunk[2]:
                term[g, 0, :, :, where] = new[:half_rows].reshape(length, rows, unit)
                ysend[g, :, :, where] = new[half_rows:].reshape(length, rows, unit).astype(
                    ysend.dtype)
            else:
                term[g, :, :, :, where] = new.reshape(2, length, rows, unit)

        tiles(chunk, body)

    def send_across(g, c):
        for delta in range(length - 1, 0, -1):
            @pl.when(z + delta < length)
            def _():
                r_y(g, c, z + delta).start()

            @pl.when(z - delta >= 0)
            def _():
                r_y(g, c, z - delta).start()
        r_y(g, c, z).start()

    def fold(g, f, delta):
        c, lane = scatter_flows[g][f]
        chunk = scatter_plan[g][c]
        for d in range(2):
            block = z + delta if d == 0 else z - delta

            def run(arrived):
                def body(where):
                    new = term[g, lane, block, :, where]
                    if chunk[2]:
                        new = new + yrecv[g, block, :, where].astype(jnp.float32)
                    if arrived:
                        new = new + slot[g, lane, block, :, where].astype(jnp.float32)
                    slot[g, lane, block, :, where] = new.astype(slot.dtype)

                tiles(chunk, body)

            @pl.when(block < length if d == 0 else block >= 0)
            def _():
                if chunk[2]:
                    r_y(g, c, block).wait_recv()
                if delta < length - 1:
                    @pl.when(can[1 - d])
                    def _():
                        r_z(g, f, block, d, False).wait_recv()
                        run(True)

                    @pl.when(jnp.logical_not(can[1 - d]))
                    def _():
                        run(False)
                else:
                    run(False)
                r_z(g, f, block, d, delta == 1).start()

    def scatter_open(g):
        plan = scatter_plan[g]
        for c in doubles(plan):
            apply(g, c)
        scatter_double(g, length - 1)
        for c in singles(plan):
            apply(g, c)
            send_across(g, c)

    def scatter_double(g, delta):
        for f, (c, _) in enumerate(scatter_flows[g]):
            if not scatter_plan[g][c][2]:
                fold(g, f, delta)

    def scatter_single(g, delta):
        for f, (c, _) in enumerate(scatter_flows[g]):
            if scatter_plan[g][c][2]:
                fold(g, f, delta)

    def result(g, c):
        start, size, _ = scatter_plan[g][c]
        piece = yrecv.at[g, z, :, pl.ds(start, size)]
        here = pl.ds(g // 2 * rows, rows)
        return (pltpu.make_async_copy(piece, out.at[here, span(core, start, size)],
                                      out_local.at[g, c]),
                remote(piece, out.at[here, span(core, start, size)], out_sem.at[0, g, c],
                       out_sem.at[1, g, c], peer),
                remote(piece, out.at[here, span(other, start, size)], out_sem.at[0, g, c],
                       out_sem.at[1, g, c], peer))

    def collect(g, f):
        c, lane = scatter_flows[g][f]
        chunk = scatter_plan[g][c]
        for d in range(2):
            lands = length if d else z

            @pl.when(can[1 - d])
            def _():
                r_z(g, f, z, d, True).wait_recv()

                def body(where):
                    term[g, lane, z, :, where] = (
                        term[g, lane, z, :, where]
                        + slot[g, lane, lands, :, where].astype(jnp.float32))

                tiles(chunk, body)

    def collect_across(g):
        for f, (c, lane) in enumerate(scatter_flows[g]):
            if lane:
                collect(g, f)

                def body(where):
                    ysend[g, z, :, where] = term[g, 1, z, :, where].astype(ysend.dtype)

                tiles(scatter_plan[g][c], body)
                r_y(g, c, z).start()

    def collect_own(g, single):
        for f, (c, lane) in enumerate(scatter_flows[g]):
            if lane == 0 and scatter_plan[g][c][2] == single:
                collect(g, f)
                r_y(g, c, z).wait_recv()

                def body(where):
                    new = term[g, 0, z, :, where] + yrecv[g, z, :, where].astype(jnp.float32)
                    yrecv[g, z, :, where] = new.astype(yrecv.dtype)

                tiles(scatter_plan[g][c], body)
                local, far, _ = result(g, c)

                @pl.when(core == g % 2)
                def _():
                    local.start()

                @pl.when(core != g % 2)
                def _():
                    far.start()

    def entered(sub):
        own_copies[sub].wait()
        peer_in[sub].wait_recv()

    entered(0)
    gather_open(0, False)

    mine = pl.ds(pl.multiple_of(core * depth, depth), depth)
    theirs = pl.ds(pl.multiple_of(other * depth, depth), depth)
    proj_local = pltpu.make_async_copy(proj.at[:, span(core, 0, width)], full.at[mine, :],
                                       own_sem.at[groups // 2])
    proj_local.start()
    proj_out = remote(proj.at[:, span(other, 0, width)], full.at[mine, :], proj_sem.at[0],
                      proj_sem.at[1], peer)
    proj_out.start()
    proj_in = remote(proj.at[:, span(other, 0, width)], full.at[theirs, :], proj_sem.at[0],
                     proj_sem.at[1], peer)
    mixes[core] = mix_matrix(table, index[...], count[...])
    mix_out = remote(mixes.at[core], mixes.at[core], mix_sem.at[0], mix_sem.at[1], peer)
    mix_out.start()
    mix_in = remote(mixes.at[other], mixes.at[other], mix_sem.at[0], mix_sem.at[1], peer)
    for sub in range(1, groups // 2):
        entered(sub)

    gather_step(0, 1)
    gather_early(1)
    for delta in range(2, length):
        gather_step(0, delta)
    for delta in range(1, length):
        gather_double(0, delta)
    gather_open(1, True)
    proj_local.wait()
    proj_in.wait_recv()
    mix_in.wait_recv()
    gather_close(0)
    meet(0)
    core_sum(0).start()

    for g in range(groups):
        more = g + 1 < groups
        middle_two(g)
        if more:
            gather_step(g + 1, 1)
            if g + 2 < groups:
                gather_early(g + 2)
        if g:
            scatter_single(g - 1, 1)
        middle_three(g)
        share(g, give).wait_recv()
        scatter_open(g)
        if g:
            collect_across(g - 1)
            collect_own(g - 1, True)
        for delta in range(length - 2, 0, -1):
            if more:
                gather_step(g + 1, length - delta)
            scatter_double(g, delta)
        if g:
            collect_own(g - 1, False)
        for delta in range(length - 1, 1, -1):
            if more:
                gather_double(g + 1, length - delta)
            scatter_single(g, delta)
        if more:
            gather_double(g + 1, length - 1)
            if g + 2 < groups:
                gather_open(g + 2, True)
            gather_close(g + 1)
            meet(g + 1)
            core_sum(g + 1).start()

    collect_across(groups - 1)
    scatter_single(groups - 1, 1)
    collect_own(groups - 1, False)
    collect_own(groups - 1, True)

    for sub in range(groups // 2):
        peer_out[sub].wait_send()
    proj_out.wait_send()
    mix_out.wait_send()
    for g in range(groups):
        share(g, keep).wait_send()
        for f, (c, lane) in enumerate(gather_flows[g]):
            @pl.loop(0, length)
            def _(block):
                @pl.when((block <= z) & can[0])
                def _():
                    a_z(g, f, block, 0).wait_send()

                @pl.when((block > z) & can[1])
                def _():
                    a_z(g, f, block, 1).wait_send()

            @pl.when(can[1])
            def _():
                a_z(g, f, z, 1, True).wait_send()
        for f in range(len(scatter_flows[g])):
            @pl.loop(0, length)
            def _(block):
                @pl.when(block != z)
                def _():
                    r_z(g, f, block, 0, False).wait_send()
        for c, chunk in enumerate(gather_plan[g]):
            if chunk[2]:
                @pl.loop(0, length)
                def _(block):
                    a_y(g, c, block).wait_send()
            else:
                a_y(g, c, z).wait_send()
        for c, chunk in enumerate(scatter_plan[g]):
            if chunk[2]:
                @pl.loop(0, length)
                def _(block):
                    r_y(g, c, block).wait_send()
            else:
                r_y(g, c, z).wait_send()
            local, far, coming = result(g, c)

            @pl.when(core == g % 2)
            def _():
                local.wait()
                coming.wait_recv()

            @pl.when(core != g % 2)
            def _():
                far.wait_send()


def shards(chips, bands, wave_rows, projectors, dij_table, dij_index, proj_count):
    depth = dij_index.shape[0] * dij_table.shape[1]
    all_rows, columns = wave_rows.shape
    length = chips // 2
    width = columns // 2
    both = 2 * depth
    groups = GROUPS
    rows = 2 * all_rows // groups
    others = max(bands - 1, 1)
    gather_plan = [chunks_of(width, share) for share in GATHER_SHARE]
    scatter_plan = [chunks_of(width, share) for share in SCATTER_SHARE]
    chunks = max(len(p) for p in gather_plan + scatter_plan)
    flows = max(len(flows_of(p)) for p in gather_plan + scatter_plan)
    dma = pltpu.SemaphoreType.DMA
    f32, bf16 = jnp.float32, jnp.bfloat16
    anywhere = pl.BlockSpec(memory_space=pl.ANY)
    return pl.pallas_call(
        functools.partial(kernel, length, bands, gather_plan, scatter_plan),
        out_shape=jax.ShapeDtypeStruct((all_rows, columns), bf16),
        in_specs=[anywhere, anywhere] + [pl.BlockSpec(memory_space=pltpu.VMEM)] * 3,
        out_specs=anywhere,
        scratch_shapes=[
            pltpu.VMEM((groups, 2, length, rows, width), bf16),
            pltpu.VMEM((both, width), bf16),
            pltpu.VMEM((groups, 2, length, rows, width), f32),
            pltpu.VMEM((groups, length, rows, width), bf16),
            pltpu.VMEM((groups, length, rows, width), bf16),
            pltpu.VMEM((groups, 2, length + 1, rows, width), bf16),
            pltpu.VMEM((groups, 2, length * rows, both), f32),
            pltpu.VMEM((groups, length * rows, both), f32),
            pltpu.VMEM((groups, others, length * rows, both), f32),
            pltpu.VMEM((2, depth, depth), f32),
            pltpu.VMEM((groups, 2, length * rows, both), bf16),
            dma((groups // 2 + 1,)), dma((2, groups // 2)), dma((2,)), dma((2,)),
            dma((groups, flows, length + 1)), dma((groups, flows, length)),
            dma((groups, chunks, length)), dma((groups, chunks, length)),
            dma((groups, flows, length)), dma((groups, flows, length + 1)),
            dma((groups, chunks, length)), dma((groups, chunks, length)),
            dma((2, groups)), dma((groups, others)), dma((groups, others)), dma((2, groups)),
            dma((2, groups, chunks)), dma((groups, chunks)),
        ],
        compiler_params=pltpu.CompilerParams(
            collective_id=0, has_side_effects=True, vmem_limit_bytes=60 * 1024 * 1024
        ),
    )(wave_rows, projectors, dij_table, dij_index[:, None], proj_count[:, None])


def solution(mesh):
    in_specs = (P("atom", "band"), P("atom", "band"), P(), P("atom"), P("atom"))
    chips = mesh.shape["atom"] // 2
    bands = mesh.shape["band"]
    return jax.jit(
        jax.shard_map(
            functools.partial(shards, chips, bands),
            mesh=mesh,
            in_specs=in_specs,
            out_specs=P("atom", "band"),
            check_vma=False,
        )
    )
```

time: 185 us -> 220 us (1.19)
  Pallas kernels: 179 us -> 212 us
    pallas_call x1, Pallas kernels: 179 us -> 212 us  [shards(): pl.pallas_call(functools.partial(kernel, length, bands, gather_plan, scat...]
where the time goes in v1:
time: 220 us; the launch traced here: 219 us
  Pallas kernels  212 us (96%)
  local copies, waits for them, and re-layouts  6.38 us (3%)
    pallas_call x1, Pallas kernels, shards(): pl.pallas_call(functools.partial(kernel, length, bands, gather_plan, scat...  212 us

profile of v1, /device:TPU:0, one launch (start us, length us, event | category | flops | bytes accessed | tf_op | source)
XLA Modules:
  0.0 218.5 jit_solution(11539235319250892743)
XLA Ops:
  0.0 1.3 copy.7.index
  1.3 1.3 copy.8.count
  2.6 1.5 copy.6.table
  4.1 212.1 %shard_map.68 = bf16[16,32768]{1,0:T(8,128)(2,1)} custom-call(bf16[16,32768]{1,0:T(8,128)(2,1)} %wave.1, bf16[128,32768]{1,0:T(8,128)(2,1)} %proj.1, f32[16,8,8]{2,1,0:T(8,128)} %copy.6.table, s32[16,1]{1,0:T(8,128)} %copy.7.index, s32[16,1]{1,0:T(8,128)} %copy.8.count), custom_call_target="tpu_custom_call" | custom-call | tf_op jit(solution)/jit(shards)/shard_map/pallas_call | solution.py:549
  216.3 2.3 %copy.10 = bf16[16,32768]{1,0:T(8,128)(2,1)} copy(bf16[16,32768]{1,0:T(8,128)(2,1)} %shard_map.68) | data formatting | bytes 2097152

commit v2 on v1

--- a/solution.py
+++ b/solution.py
@@ -8,9 +8,11 @@
 from jax.sharding import PartitionSpec as P
 
 MESH = pl.DeviceIdType.MESH
-GROUPS = 2
-GATHER_SHARE = (0.8125, 0.5)
-SCATTER_SHARE = (0.5, 0.8125)
+GROUPS = 4
+ANY, EDGE, INNER = range(3)
+GATHER_SHARE = (0.8125, 0.625, 0.5625, 0.5625)
+SCATTER_SHARE = (0.5625, 0.5625, 0.625, 0.8125)
+PARTS = (2, 1)
 
 
 def mix_matrix(table, index, count):
@@ -49,8 +51,12 @@
     unit = max(width // 32, 128)
     units = width // unit
     single = min(max(round(share * units), 1), units)
-    first = (single + 1) // 2
-    cuts = [(0, first, True), (first, single - first, True), (single, units - single, False)]
+    cuts = []
+    for at, size, parts, kind in ((0, single, PARTS[0], True),
+                                  (single, units - single, PARTS[1], False)):
+        for p in range(parts):
+            low, high = size * p // parts, size * (p + 1) // parts
+            cuts.append((at + low, high - low, kind))
     return [(start * unit, size * unit, kind) for start, size, kind in cuts if size]
 
 
@@ -59,8 +65,214 @@
             + [(c, lane) for c, chunk in enumerate(chunks) if not chunk[2] for lane in range(2)])
 
 
-def kernel(length, bands, gather_plan, scatter_plan, wave, proj, table, index, count, out, gath,
-           full, term, ysend, yrecv, slot, inter, swap, parts, mixes, weights, own_sem, wave_sem,
+SLOTS = [
+    ("az", 3, 1, 0, EDGE, [0]),
+    ("az", 0, 1, 0, ANY, [1]),
+    ("ay", 0, 2, [2]),
+    ("az", 0, 1, 1, ANY, [3]),
+    ("az", 0, 0, 0, ANY, [4]),
+    ("az", 2, 1, 0, EDGE, [5]),
+    ("az", 2, 1, 1, EDGE, [6]),
+    ("az", 0, 0, 1, ANY, [7]),
+    ("ay", 2, 2, [8]),
+    ("ay", 0, 1, [9]),
+    ("ew", 0, 2, [10]),
+    ("az", 0, 2, 0, ANY, [11]),
+    ("az", 1, 1, 0, EDGE, [12]),
+    ("az", 0, 3, 1, ANY, [13]),
+    ("ar", 0, 1, 1, [14, 23, 26]),
+    ("ar", 0, 1, 0, [15, 21, 27]),
+    ("az", 2, 0, 1, INNER, [16]),
+    ("ar", 0, 0, 0, [17, 32, 35]),
+    ("az", 0, 2, 1, ANY, [18]),
+    ("az", 2, 0, 0, EDGE, [19]),
+    ("az", 0, 3, 0, ANY, [20]),
+    ("ay", 0, 0, [22]),
+    ("ar", 0, 2, 0, [24, 36, 41]),
+    ("ar", 0, 0, 1, [25, 29, 37]),
+    ("ar", 0, 3, 1, [28, 40, 60]),
+    ("az", 1, 0, 1, EDGE, [30]),
+    ("az", 1, 0, 0, EDGE, [31]),
+    ("ar", 0, 2, 1, [33, 39, 62]),
+    ("az", 3, 0, 1, EDGE, [34]),
+    ("ew", 2, 2, [38]),
+    ("az", 2, 0, 1, EDGE, [42]),
+    ("ay", 1, 2, [43]),
+    ("ar", 0, 3, 0, [44, 48, 51]),
+    ("az", 2, 1, 1, INNER, [45]),
+    ("az", 2, 1, 0, INNER, [46]),
+    ("az", 2, 0, 0, INNER, [47]),
+    ("az", 1, 2, 0, ANY, [49]),
+    ("az", 2, 2, 1, ANY, [50]),
+    ("ay", 2, 1, [52]),
+    ("az", 2, 3, 1, ANY, [53]),
+    ("ar", 2, 1, 0, [54, 85, 101]),
+    ("az", 3, 0, 0, EDGE, [55]),
+    ("az", 2, 2, 0, ANY, [56]),
+    ("ar", 2, 0, 1, [57, 79, 97]),
+    ("ar", 2, 1, 1, [58, 76, 89]),
+    ("az", 1, 1, 1, EDGE, [59]),
+    ("close", 0, [61]),
+    ("ar", 2, 0, 0, [63, 75, 91]),
+    ("ay", 3, 1, [64]),
+    ("ay", 3, 2, [65]),
+    ("az", 2, 3, 0, ANY, [66]),
+    ("meet", 0, [67]),
+    ("ay", 2, 0, [68]),
+    ("az", 3, 1, 1, EDGE, [69]),
+    ("ar", 2, 2, 1, [70, 81, 108]),
+    ("ay", 1, 1, [71]),
+    ("ar", 2, 3, 1, [72, 82, 120]),
+    ("ar", 2, 2, 0, [73, 96, 115]),
+    ("m2", 0, [74]),
+    ("m3", 0, [77]),
+    ("ew", 1, 2, [78]),
+    ("ar", 2, 3, 0, [80, 95, 112]),
+    ("az", 3, 2, 1, ANY, [83]),
+    ("sh", 0, [84]),
+    ("az", 1, 0, 1, INNER, [86]),
+    ("ap", 0, 2, [87]),
+    ("az", 1, 1, 1, INNER, [88]),
+    ("fo", 0, 3, 0, [207, 109, 90]),
+    ("ew", 3, 2, [92]),
+    ("fo", 0, 3, 1, [218, 114, 93]),
+    ("ap", 0, 0, [94]),
+    ("az", 3, 3, 1, ANY, [98]),
+    ("fo", 0, 2, 1, [228, 133, 99]),
+    ("ys", 0, 0, [121, 110, 100]),
+    ("ap", 0, 1, [102]),
+    ("ys", 0, 1, [126, 103, 113]),
+    ("fo", 0, 0, 1, [220, 128, 104]),
+    ("az", 1, 3, 1, ANY, [105]),
+    ("az", 1, 3, 0, ANY, [106]),
+    ("az", 3, 2, 0, ANY, [107]),
+    ("az", 1, 0, 0, INNER, [111]),
+    ("az", 1, 1, 0, INNER, [116]),
+    ("fo", 0, 2, 0, [191, 144, 117]),
+    ("yo", 0, 0, [118]),
+    ("az", 1, 2, 1, ANY, [119]),
+    ("close", 2, [122]),
+    ("meet", 2, [123]),
+    ("fo", 0, 1, 0, [222, 142, 124]),
+    ("ar", 1, 0, 1, [125, 150, 173]),
+    ("ar", 1, 1, 1, [127, 163, 176]),
+    ("az", 3, 1, 1, INNER, [129]),
+    ("ar", 1, 0, 0, [130, 136, 154]),
+    ("m2", 2, [131]),
+    ("ar", 1, 1, 0, [132, 145, 180]),
+    ("az", 3, 3, 0, ANY, [134]),
+    ("fo", 0, 0, 0, [224, 177, 135]),
+    ("ay", 1, 0, [137]),
+    ("fo", 0, 1, 1, [225, 146, 138]),
+    ("ar", 1, 2, 0, [139, 170, 203]),
+    ("m3", 2, [140]),
+    ("ar", 1, 3, 0, [141, 172, 206]),
+    ("ar", 1, 3, 1, [143, 181, 198]),
+    ("sh", 2, [147]),
+    ("ap", 2, 2, [148]),
+    ("az", 3, 0, 0, INNER, [149]),
+    ("ar", 1, 2, 1, [151, 178, 193]),
+    ("fo", 2, 2, 1, [204, 165, 152]),
+    ("fo", 2, 2, 0, [214, 164, 153]),
+    ("fo", 2, 3, 1, [200, 171, 155]),
+    ("az", 3, 0, 1, INNER, [156]),
+    ("ap", 2, 0, [157]),
+    ("ys", 2, 0, [182, 162, 158]),
+    ("fo", 2, 3, 0, [226, 167, 159]),
+    ("ap", 2, 1, [160]),
+    ("ys", 2, 1, [190, 168, 161]),
+    ("az", 3, 1, 0, INNER, [166]),
+    ("fo", 2, 0, 0, [245, 192, 169]),
+    ("fo", 2, 1, 0, [229, 202, 174]),
+    ("fo", 2, 0, 1, [217, 195, 175]),
+    ("fo", 2, 1, 1, [242, 201, 179]),
+    ("ar", 3, 1, 0, [183, 210, 239]),
+    ("ar", 3, 0, 0, [184, 209, 234]),
+    ("ar", 3, 3, 0, [185, 219, 256]),
+    ("yo", 2, 0, [186]),
+    ("ar", 3, 2, 1, [187, 215, 243]),
+    ("ar", 3, 2, 0, [188, 221, 259]),
+    ("ar", 3, 1, 1, [189, 212, 231]),
+    ("ar", 3, 0, 1, [194, 213, 236]),
+    ("yo", 2, 1, [196]),
+    ("ar", 3, 3, 1, [197, 216, 253]),
+    ("ay", 3, 0, [199]),
+    ("close", 1, [205]),
+    ("meet", 1, [208]),
+    ("yo", 0, 1, [211]),
+    ("m2", 1, [223]),
+    ("m3", 1, [227]),
+    ("sh", 1, [230]),
+    ("ap", 1, 2, [232]),
+    ("fo", 1, 3, 0, [263, 246, 233]),
+    ("fo", 1, 3, 1, [264, 251, 235]),
+    ("ap", 1, 0, [237]),
+    ("ys", 1, 0, [247, 250, 238]),
+    ("fo", 1, 2, 1, [272, 252, 240]),
+    ("fo", 1, 2, 0, [314, 257, 241]),
+    ("ap", 1, 1, [244]),
+    ("ys", 1, 1, [255, 258, 248]),
+    ("yo", 1, 0, [249]),
+    ("fo", 1, 0, 1, [283, 271, 254]),
+    ("close", 3, [260]),
+    ("meet", 3, [261]),
+    ("fo", 1, 0, 0, [285, 270, 262]),
+    ("fo", 1, 1, 1, [294, 276, 265]),
+    ("m2", 3, [266]),
+    ("yo", 1, 1, [267]),
+    ("fo", 1, 1, 0, [288, 275, 268]),
+    ("ca", 2, 3, [269]),
+    ("ca", 0, 3, [273]),
+    ("m3", 3, [274]),
+    ("co", 2, 1, [277]),
+    ("sh", 3, [278]),
+    ("ap", 3, 1, [279]),
+    ("ys", 3, 1, [291, 282, 280]),
+    ("ap", 3, 2, [281]),
+    ("fo", 3, 2, 1, [327, 296, 284]),
+    ("ap", 3, 0, [286]),
+    ("fo", 3, 3, 0, [307, 292, 287]),
+    ("ys", 3, 0, [301, 290, 289]),
+    ("fo", 3, 3, 1, [318, 309, 293]),
+    ("fo", 3, 1, 0, [317, 305, 295]),
+    ("fo", 3, 2, 0, [324, 312, 297]),
+    ("co", 0, 0, [298]),
+    ("co", 0, 2, [299]),
+    ("fo", 3, 1, 1, [319, 313, 300]),
+    ("ca", 1, 3, [302]),
+    ("fo", 3, 0, 0, [320, 311, 303]),
+    ("fo", 3, 0, 1, [323, 315, 304]),
+    ("co", 2, 2, [306]),
+    ("co", 0, 1, [308]),
+    ("yo", 3, 1, [310]),
+    ("co", 2, 0, [316]),
+    ("yo", 3, 0, [321]),
+    ("co", 1, 0, [322]),
+    ("co", 1, 1, [325]),
+    ("ca", 3, 3, [326]),
+    ("co", 3, 1, [328]),
+    ("co", 1, 2, [329]),
+    ("co", 3, 0, [330]),
+    ("co", 3, 2, [331]),
+]
+
+
+def order_of(length):
+    keyed = []
+    for name, group, *rest, slots in SLOTS:
+        if len(slots) == 1:
+            keyed.append((slots[0], (name, group, *rest)))
+            continue
+        for delta in range(1, length):
+            at = (delta - 1) * (len(slots) - 1) / max(length - 2, 1)
+            low = min(int(at), len(slots) - 2)
+            key = slots[low] + (at - low) * (slots[low + 1] - slots[low])
+            keyed.append((key, (name, group, delta, *rest)))
+    return [step for _, step in sorted(keyed, key=lambda pair: pair[0])]
+
+
+def kernel(length, bands, gather_plan, scatter_plan, steps, wave, proj, table, index, count, out,
+           gath, full, term, ysend, yrecv, slot, inter, swap, parts, mixes, weights, own_sem, wave_sem,
            proj_sem, mix_sem, az_s, az_r, ay_s, ay_r, rz_s, rz_r, ry_s, ry_r, swap_sem, part_s,
            part_r, wt_sem, out_sem, out_local):
     atom = lax.axis_index("atom")
@@ -122,12 +334,6 @@
     gather_flows = [flows_of(p) for p in gather_plan]
     scatter_flows = [flows_of(p) for p in scatter_plan]
 
-    def singles(plan):
-        return [c for c, chunk in enumerate(plan) if chunk[2]]
-
-    def doubles(plan):
-        return [c for c, chunk in enumerate(plan) if not chunk[2]]
-
     def cols(chunk):
         return pl.ds(chunk[0], chunk[1])
 
@@ -142,69 +348,53 @@
         return remote(gath.at[g, 0, block, :, where], gath.at[g, 1, block, :, where],
                       ay_s.at[g, c, block], ay_r.at[g, c, block], across)
 
-    def own_z(g, d, when, single, lane=0):
-        for f, (c, on) in enumerate(gather_flows[g]):
-            if gather_plan[g][c][2] == single and on == lane:
-                @pl.when(when)
-                def _():
-                    a_z(g, f, z, d, True).start()
-
-    def own_y(g, single):
-        for c in (singles if single else doubles)(gather_plan[g]):
-            a_y(g, c, z).start()
-
-    def arrive(g, f, delta):
+    def start_across(g, c):
+        a_y(g, c, z).start()
+
+    def start_along(g, f, d, part):
+        when = can[d]
+        if part == EDGE:
+            when = when & edge[d]
+        if part == INNER:
+            when = when & jnp.logical_not(edge[d])
+
+        @pl.when(when)
+        def _():
+            a_z(g, f, z, d, True).start()
+
+    def enter(g, c):
+        a_y(g, c, z).wait_recv()
+
+    def arrive(g, delta, f, d):
         c, _ = gather_flows[g][f]
-        for d in range(2):
-            block = z - delta if d == 0 else z + delta
-
-            @pl.when(block >= 0 if d == 0 else block < length)
+        block = z - delta if d == 0 else z + delta
+
+        @pl.when(block >= 0 if d == 0 else block < length)
+        def _():
+            copy = a_z(g, f, block, d)
+            copy.wait_recv()
+
+            @pl.when(can[d])
             def _():
-                copy = a_z(g, f, block, d)
-                copy.wait_recv()
-
-                @pl.when(can[d])
-                def _():
-                    copy.start()
-                if gather_plan[g][c][2]:
-                    a_y(g, c, block).start()
-
-    def gather_early(g):
-        for d in range(2):
-            own_z(g, d, can[d] & edge[d], True)
-
-    def gather_open(g, early):
-        own_y(g, False)
-        for d in range(2):
-            own_z(g, d, can[d] & jnp.logical_not(edge[d]) if early else can[d], True)
-        own_y(g, True)
-
-    def gather_step(g, delta):
-        for f, (c, _) in enumerate(gather_flows[g]):
+                copy.start()
             if gather_plan[g][c][2]:
-                arrive(g, f, delta)
-        if delta == 1:
-            for d in range(2):
-                own_z(g, d, can[d], False)
-            for c in doubles(gather_plan[g]):
-                a_y(g, c, z).wait_recv()
-            for d in range(2):
-                own_z(g, d, can[d], False, 1)
-
-    def gather_double(g, delta):
-        for f, (c, _) in enumerate(gather_flows[g]):
-            if not gather_plan[g][c][2]:
-                arrive(g, f, delta)
+                a_y(g, c, block).start()
 
     def gather_close(g):
-        for c in singles(gather_plan[g]):
-            for block in range(length):
-                a_y(g, c, block).wait_recv()
+        for c, chunk in enumerate(gather_plan[g]):
+            if chunk[2]:
+                for block in range(length):
+                    a_y(g, c, block).wait_recv()
 
     kt = min(1024, width)
     keep, give = core, other
 
     def meet(g):
+        if g == 0:
+            proj_local.wait()
+            proj_in.wait_recv()
+            mix_in.wait_recv()
+
         def body(t, acc):
             where = pl.ds(pl.multiple_of(t * kt, kt), kt)
             left = gath[g, :, :, :, where].reshape(2 * half_rows, kt)
@@ -213,6 +403,7 @@
 
         total = lax.fori_loop(0, width // kt, body, jnp.zeros((2 * half_rows, both), jnp.float32))
         inter[g] = total.reshape(2, half_rows, both)
+        core_sum(g).start()
 
     def core_sum(g):
         return remote(inter.at[g, give], swap.at[g], swap_sem.at[0, g], swap_sem.at[1, g], peer)
@@ -244,6 +435,9 @@
                 preferred_element_type=jnp.float32).astype(weights.dtype)
         share(g, keep).start()
 
+    def shared(g):
+        share(g, give).wait_recv()
+
     def r_y(g, c, block):
         where = cols(scatter_plan[g][c])
         return remote(ysend.at[g, block, :, where], yrecv.at[g, block, :, where],
@@ -278,69 +472,47 @@
 
         tiles(chunk, body)
 
-    def send_across(g, c):
-        for delta in range(length - 1, 0, -1):
-            @pl.when(z + delta < length)
+    def send_own_across(g, c):
+        r_y(g, c, z).start()
+
+    def send_across(g, delta, c):
+        for block in (z + delta, z - delta):
+            @pl.when((block >= 0) & (block < length))
             def _():
-                r_y(g, c, z + delta).start()
-
-            @pl.when(z - delta >= 0)
-            def _():
-                r_y(g, c, z - delta).start()
-        r_y(g, c, z).start()
-
-    def fold(g, f, delta):
+                r_y(g, c, block).start()
+
+    def fold(g, delta, f, d):
         c, lane = scatter_flows[g][f]
         chunk = scatter_plan[g][c]
-        for d in range(2):
-            block = z + delta if d == 0 else z - delta
-
-            def run(arrived):
-                def body(where):
-                    new = term[g, lane, block, :, where]
-                    if chunk[2]:
-                        new = new + yrecv[g, block, :, where].astype(jnp.float32)
-                    if arrived:
-                        new = new + slot[g, lane, block, :, where].astype(jnp.float32)
-                    slot[g, lane, block, :, where] = new.astype(slot.dtype)
-
-                tiles(chunk, body)
-
-            @pl.when(block < length if d == 0 else block >= 0)
-            def _():
+        block = z + delta if d == 0 else z - delta
+
+        def run(arrived):
+            def body(where):
+                new = term[g, lane, block, :, where]
                 if chunk[2]:
-                    r_y(g, c, block).wait_recv()
-                if delta < length - 1:
-                    @pl.when(can[1 - d])
-                    def _():
-                        r_z(g, f, block, d, False).wait_recv()
-                        run(True)
-
-                    @pl.when(jnp.logical_not(can[1 - d]))
-                    def _():
-                        run(False)
-                else:
+                    new = new + yrecv[g, block, :, where].astype(jnp.float32)
+                if arrived:
+                    new = new + slot[g, lane, block, :, where].astype(jnp.float32)
+                slot[g, lane, block, :, where] = new.astype(slot.dtype)
+
+            tiles(chunk, body)
+
+        @pl.when(block < length if d == 0 else block >= 0)
+        def _():
+            if chunk[2]:
+                r_y(g, c, block).wait_recv()
+            if delta < length - 1:
+                @pl.when(can[1 - d])
+                def _():
+                    r_z(g, f, block, d, False).wait_recv()
+                    run(True)
+
+                @pl.when(jnp.logical_not(can[1 - d]))
+                def _():
                     run(False)
-                r_z(g, f, block, d, delta == 1).start()
-
-    def scatter_open(g):
-        plan = scatter_plan[g]
-        for c in doubles(plan):
-            apply(g, c)
-        scatter_double(g, length - 1)
-        for c in singles(plan):
-            apply(g, c)
-            send_across(g, c)
-
-    def scatter_double(g, delta):
-        for f, (c, _) in enumerate(scatter_flows[g]):
-            if not scatter_plan[g][c][2]:
-                fold(g, f, delta)
-
-    def scatter_single(g, delta):
-        for f, (c, _) in enumerate(scatter_flows[g]):
-            if scatter_plan[g][c][2]:
-                fold(g, f, delta)
+            else:
+                run(False)
+            r_z(g, f, block, d, delta == 1).start()
 
     def result(g, c):
         start, size, _ = scatter_plan[g][c]
@@ -370,113 +542,71 @@
 
                 tiles(chunk, body)
 
-    def collect_across(g):
-        for f, (c, lane) in enumerate(scatter_flows[g]):
-            if lane:
-                collect(g, f)
-
-                def body(where):
-                    ysend[g, z, :, where] = term[g, 1, z, :, where].astype(ysend.dtype)
-
-                tiles(scatter_plan[g][c], body)
-                r_y(g, c, z).start()
-
-    def collect_own(g, single):
-        for f, (c, lane) in enumerate(scatter_flows[g]):
-            if lane == 0 and scatter_plan[g][c][2] == single:
-                collect(g, f)
-                r_y(g, c, z).wait_recv()
-
-                def body(where):
-                    new = term[g, 0, z, :, where] + yrecv[g, z, :, where].astype(jnp.float32)
-                    yrecv[g, z, :, where] = new.astype(yrecv.dtype)
-
-                tiles(scatter_plan[g][c], body)
-                local, far, _ = result(g, c)
-
-                @pl.when(core == g % 2)
-                def _():
-                    local.start()
-
-                @pl.when(core != g % 2)
-                def _():
-                    far.start()
+    def collect_across(g, f):
+        c, _ = scatter_flows[g][f]
+        collect(g, f)
+
+        def body(where):
+            ysend[g, z, :, where] = term[g, 1, z, :, where].astype(ysend.dtype)
+
+        tiles(scatter_plan[g][c], body)
+        r_y(g, c, z).start()
+
+    def collect_own(g, f):
+        c, _ = scatter_flows[g][f]
+        collect(g, f)
+        r_y(g, c, z).wait_recv()
+
+        def body(where):
+            new = term[g, 0, z, :, where] + yrecv[g, z, :, where].astype(jnp.float32)
+            yrecv[g, z, :, where] = new.astype(yrecv.dtype)
+
+        tiles(scatter_plan[g][c], body)
+        local, far, _ = result(g, c)
+
+        @pl.when(core == g % 2)
+        def _():
+            local.start()
+
+        @pl.when(core != g % 2)
+        def _():
+            far.start()
 
     def entered(sub):
         own_copies[sub].wait()
         peer_in[sub].wait_recv()
 
-    entered(0)
-    gather_open(0, False)
-
+    run = dict(
+        ay=start_across, az=start_along, ew=enter, ar=arrive, close=gather_close, meet=meet,
+        m2=middle_two, m3=middle_three, sh=shared, ap=apply, ys=send_across,
+        yo=send_own_across, fo=fold, ca=collect_across, co=collect_own)
     mine = pl.ds(pl.multiple_of(core * depth, depth), depth)
     theirs = pl.ds(pl.multiple_of(other * depth, depth), depth)
     proj_local = pltpu.make_async_copy(proj.at[:, span(core, 0, width)], full.at[mine, :],
                                        own_sem.at[groups // 2])
-    proj_local.start()
     proj_out = remote(proj.at[:, span(other, 0, width)], full.at[mine, :], proj_sem.at[0],
                       proj_sem.at[1], peer)
-    proj_out.start()
     proj_in = remote(proj.at[:, span(other, 0, width)], full.at[theirs, :], proj_sem.at[0],
                      proj_sem.at[1], peer)
-    mixes[core] = mix_matrix(table, index[...], count[...])
     mix_out = remote(mixes.at[core], mixes.at[core], mix_sem.at[0], mix_sem.at[1], peer)
-    mix_out.start()
     mix_in = remote(mixes.at[other], mixes.at[other], mix_sem.at[0], mix_sem.at[1], peer)
-    for sub in range(1, groups // 2):
-        entered(sub)
-
-    gather_step(0, 1)
-    gather_early(1)
-    for delta in range(2, length):
-        gather_step(0, delta)
-    for delta in range(1, length):
-        gather_double(0, delta)
-    gather_open(1, True)
-    proj_local.wait()
-    proj_in.wait_recv()
-    mix_in.wait_recv()
-    gather_close(0)
-    meet(0)
-    core_sum(0).start()
-
-    for g in range(groups):
-        more = g + 1 < groups
-        middle_two(g)
-        if more:
-            gather_step(g + 1, 1)
-            if g + 2 < groups:
-                gather_early(g + 2)
-        if g:
-            scatter_single(g - 1, 1)
-        middle_three(g)
-        share(g, give).wait_recv()
-        scatter_open(g)
-        if g:
-            collect_across(g - 1)
-            collect_own(g - 1, True)
-        for delta in range(length - 2, 0, -1):
-            if more:
-                gather_step(g + 1, length - delta)
-            scatter_double(g, delta)
-        if g:
-            collect_own(g - 1, False)
-        for delta in range(length - 1, 1, -1):
-            if more:
-                gather_double(g + 1, length - delta)
-            scatter_single(g, delta)
-        if more:
-            gather_double(g + 1, length - 1)
-            if g + 2 < groups:
-                gather_open(g + 2, True)
-            gather_close(g + 1)
-            meet(g + 1)
-            core_sum(g + 1).start()
-
-    collect_across(groups - 1)
-    scatter_single(groups - 1, 1)
-    collect_own(groups - 1, False)
-    collect_own(groups - 1, True)
+
+    def prepare():
+        proj_local.start()
+        proj_out.start()
+        mixes[core] = mix_matrix(table, index[...], count[...])
+        mix_out.start()
+
+    inside, prepared = set(), False
+    for name, g, *rest in steps:
+        if name in ("ay", "az"):
+            if g // 2 not in inside:
+                entered(g // 2)
+                inside.add(g // 2)
+        elif not prepared:
+            prepare()
+            prepared = True
+        run[name](g, *rest)
 
     for sub in range(groups // 2):
         peer_out[sub].wait_send()
@@ -541,13 +671,14 @@
     others = max(bands - 1, 1)
     gather_plan = [chunks_of(width, share) for share in GATHER_SHARE]
     scatter_plan = [chunks_of(width, share) for share in SCATTER_SHARE]
+    steps = order_of(length)
     chunks = max(len(p) for p in gather_plan + scatter_plan)
     flows = max(len(flows_of(p)) for p in gather_plan + scatter_plan)
     dma = pltpu.SemaphoreType.DMA
     f32, bf16 = jnp.float32, jnp.bfloat16
     anywhere = pl.BlockSpec(memory_space=pl.ANY)
     return pl.pallas_call(
-        functools.partial(kernel, length, bands, gather_plan, scatter_plan),
+        functools.partial(kernel, length, bands, gather_plan, scatter_plan, steps),
         out_shape=jax.ShapeDtypeStruct((all_rows, columns), bf16),
         in_specs=[anywhere, anywhere] + [pl.BlockSpec(memory_space=pltpu.VMEM)] * 3,
         out_specs=anywhere,

time: 220 us -> 160 us (0.73)
  Pallas kernels: 212 us -> 152 us
    pallas_call x1, Pallas kernels: 212 us -> 152 us  [shards(): pl.pallas_call(functools.partial(kernel, length, bands, gather_plan, scat...]
where the time goes in v2:
time: 160 us; the launch traced here: 159 us
  Pallas kernels  152 us (95%)
  local copies, waits for them, and re-layouts  6.38 us (4%)
    pallas_call x1, Pallas kernels, shards(): pl.pallas_call(functools.partial(kernel, length, bands, gather_plan, scat...  152 us
    unnamed x2, local copies, waits for them, and re-layouts  3.73 us

profile of v2, /device:TPU:0, one launch (start us, length us, event | category | flops | bytes accessed | tf_op | source)
XLA Modules:
  0.0 158.7 jit_solution(9927920704537418141)
XLA Ops:
  0.0 1.3 copy.7.index
  1.3 1.3 copy.8.count
  2.6 1.5 copy.6.table
  4.1 152.3 %shard_map.68 = bf16[16,32768]{1,0:T(8,128)(2,1)} custom-call(bf16[16,32768]{1,0:T(8,128)(2,1)} %wave.1, bf16[128,32768]{1,0:T(8,128)(2,1)} %proj.1, f32[16,8,8]{2,1,0:T(8,128)} %copy.6.table, s32[16,1]{1,0:T(8,128)} %copy.7.index, s32[16,1]{1,0:T(8,128)} %copy.8.count), custom_call_target="tpu_custom_call" | custom-call | tf_op jit(solution)/jit(shards)/shard_map/pallas_call | solution.py:680
  156.4 2.3 %copy.10 = bf16[16,32768]{1,0:T(8,128)(2,1)} copy(bf16[16,32768]{1,0:T(8,128)(2,1)} %shard_map.68) | data formatting | bytes 2097152

commit v3 on v2

--- a/solution.py
+++ b/solution.py
@@ -9,40 +9,35 @@
 
 MESH = pl.DeviceIdType.MESH
 GROUPS = 4
-ANY, EDGE, INNER = range(3)
-GATHER_SHARE = (0.8125, 0.625, 0.5625, 0.5625)
-SCATTER_SHARE = (0.5625, 0.5625, 0.625, 0.8125)
+GATHER_SHARE = (0.875, 0.625, 0.5625, 0.5)
+SCATTER_SHARE = (0.5, 0.5625, 0.625, 0.875)
 PARTS = (2, 1)
 
 
 def mix_matrix(table, index, count):
+    per_atom, _, kinds = table.shape
     atoms = index.shape[0]
-    kinds, per_atom = table.shape[:2]
     depth = atoms * per_atom
-    exact = functools.partial(
-        lax.dot_general, precision=lax.Precision.HIGHEST, preferred_element_type=jnp.float32)
 
     def iota(shape, axis):
         return lax.broadcasted_iota(jnp.int32, shape, axis)
 
+    def of_atom(values, shape):
+        atom_of = iota(shape, 0) // per_atom
+        spread = jnp.zeros(shape, jnp.int32)
+        for a in range(atoms):
+            spread = jnp.where(atom_of == a, values[a], spread)
+        return spread
+
     row, lane = iota((depth, depth), 0), iota((depth, depth), 1)
-    spread = (iota((depth, atoms), 0) // per_atom == iota((depth, atoms), 1)).astype(jnp.float32)
-    pick = (lax.rem(iota((depth, per_atom), 0), per_atom) == iota((depth, per_atom), 1)).astype(
-        jnp.float32)
-    plain = (((1,), (0,)), ((), ()))
-
-    def over_rows(value):
-        value = jnp.broadcast_to(value.astype(jnp.float32), (atoms, depth))
-        return exact(spread, value, plain)
-
-    kind, active = over_rows(index), over_rows(count)
+    active = of_atom(count, (depth, depth))
+    is_kind = of_atom(index, (depth, kinds)) == iota((depth, kinds), 1)
     chosen = jnp.zeros((depth, depth), jnp.float32)
-    for k in range(kinds):
-        turned = exact(pick, table[k], (((1,), (1,)), ((), ())))
-        wide = exact(turned, pick, (((1,), (1,)), ((), ())))
-        chosen = jnp.where(jnp.abs(kind - k) < 0.5, wide, chosen)
-    inside = lax.rem(row, per_atom).astype(jnp.float32) < active - 0.5
-    inside &= lax.rem(lane, per_atom).astype(jnp.float32) < active - 0.5
+    for i in range(per_atom):
+        rows = jnp.broadcast_to(table[i][None], (atoms, per_atom, kinds)).reshape(depth, kinds)
+        picked = jnp.sum(jnp.where(is_kind, rows, 0.0), axis=1, keepdims=True)
+        chosen = jnp.where(lax.rem(lane, per_atom) == i, picked, chosen)
+    inside = (lax.rem(row, per_atom) < active) & (lax.rem(lane, per_atom) < active)
     inside &= row // per_atom == lane // per_atom
     return jnp.where(inside, chosen, 0.0)
 
@@ -66,215 +61,294 @@
 
 
 SLOTS = [
-    ("az", 3, 1, 0, EDGE, [0]),
-    ("az", 0, 1, 0, ANY, [1]),
-    ("ay", 0, 2, [2]),
-    ("az", 0, 1, 1, ANY, [3]),
-    ("az", 0, 0, 0, ANY, [4]),
-    ("az", 2, 1, 0, EDGE, [5]),
-    ("az", 2, 1, 1, EDGE, [6]),
-    ("az", 0, 0, 1, ANY, [7]),
-    ("ay", 2, 2, [8]),
-    ("ay", 0, 1, [9]),
-    ("ew", 0, 2, [10]),
-    ("az", 0, 2, 0, ANY, [11]),
-    ("az", 1, 1, 0, EDGE, [12]),
-    ("az", 0, 3, 1, ANY, [13]),
-    ("ar", 0, 1, 1, [14, 23, 26]),
-    ("ar", 0, 1, 0, [15, 21, 27]),
-    ("az", 2, 0, 1, INNER, [16]),
-    ("ar", 0, 0, 0, [17, 32, 35]),
-    ("az", 0, 2, 1, ANY, [18]),
-    ("az", 2, 0, 0, EDGE, [19]),
-    ("az", 0, 3, 0, ANY, [20]),
-    ("ay", 0, 0, [22]),
-    ("ar", 0, 2, 0, [24, 36, 41]),
-    ("ar", 0, 0, 1, [25, 29, 37]),
-    ("ar", 0, 3, 1, [28, 40, 60]),
-    ("az", 1, 0, 1, EDGE, [30]),
-    ("az", 1, 0, 0, EDGE, [31]),
-    ("ar", 0, 2, 1, [33, 39, 62]),
-    ("az", 3, 0, 1, EDGE, [34]),
-    ("ew", 2, 2, [38]),
-    ("az", 2, 0, 1, EDGE, [42]),
-    ("ay", 1, 2, [43]),
-    ("ar", 0, 3, 0, [44, 48, 51]),
-    ("az", 2, 1, 1, INNER, [45]),
-    ("az", 2, 1, 0, INNER, [46]),
-    ("az", 2, 0, 0, INNER, [47]),
-    ("az", 1, 2, 0, ANY, [49]),
-    ("az", 2, 2, 1, ANY, [50]),
-    ("ay", 2, 1, [52]),
-    ("az", 2, 3, 1, ANY, [53]),
-    ("ar", 2, 1, 0, [54, 85, 101]),
-    ("az", 3, 0, 0, EDGE, [55]),
-    ("az", 2, 2, 0, ANY, [56]),
-    ("ar", 2, 0, 1, [57, 79, 97]),
-    ("ar", 2, 1, 1, [58, 76, 89]),
-    ("az", 1, 1, 1, EDGE, [59]),
-    ("close", 0, [61]),
-    ("ar", 2, 0, 0, [63, 75, 91]),
-    ("ay", 3, 1, [64]),
-    ("ay", 3, 2, [65]),
-    ("az", 2, 3, 0, ANY, [66]),
-    ("meet", 0, [67]),
-    ("ay", 2, 0, [68]),
-    ("az", 3, 1, 1, EDGE, [69]),
-    ("ar", 2, 2, 1, [70, 81, 108]),
-    ("ay", 1, 1, [71]),
-    ("ar", 2, 3, 1, [72, 82, 120]),
-    ("ar", 2, 2, 0, [73, 96, 115]),
-    ("m2", 0, [74]),
-    ("m3", 0, [77]),
-    ("ew", 1, 2, [78]),
-    ("ar", 2, 3, 0, [80, 95, 112]),
-    ("az", 3, 2, 1, ANY, [83]),
-    ("sh", 0, [84]),
-    ("az", 1, 0, 1, INNER, [86]),
-    ("ap", 0, 2, [87]),
-    ("az", 1, 1, 1, INNER, [88]),
-    ("fo", 0, 3, 0, [207, 109, 90]),
-    ("ew", 3, 2, [92]),
-    ("fo", 0, 3, 1, [218, 114, 93]),
-    ("ap", 0, 0, [94]),
-    ("az", 3, 3, 1, ANY, [98]),
-    ("fo", 0, 2, 1, [228, 133, 99]),
-    ("ys", 0, 0, [121, 110, 100]),
-    ("ap", 0, 1, [102]),
-    ("ys", 0, 1, [126, 103, 113]),
-    ("fo", 0, 0, 1, [220, 128, 104]),
-    ("az", 1, 3, 1, ANY, [105]),
-    ("az", 1, 3, 0, ANY, [106]),
-    ("az", 3, 2, 0, ANY, [107]),
-    ("az", 1, 0, 0, INNER, [111]),
-    ("az", 1, 1, 0, INNER, [116]),
-    ("fo", 0, 2, 0, [191, 144, 117]),
-    ("yo", 0, 0, [118]),
-    ("az", 1, 2, 1, ANY, [119]),
-    ("close", 2, [122]),
-    ("meet", 2, [123]),
-    ("fo", 0, 1, 0, [222, 142, 124]),
-    ("ar", 1, 0, 1, [125, 150, 173]),
-    ("ar", 1, 1, 1, [127, 163, 176]),
-    ("az", 3, 1, 1, INNER, [129]),
-    ("ar", 1, 0, 0, [130, 136, 154]),
-    ("m2", 2, [131]),
-    ("ar", 1, 1, 0, [132, 145, 180]),
-    ("az", 3, 3, 0, ANY, [134]),
-    ("fo", 0, 0, 0, [224, 177, 135]),
-    ("ay", 1, 0, [137]),
-    ("fo", 0, 1, 1, [225, 146, 138]),
-    ("ar", 1, 2, 0, [139, 170, 203]),
-    ("m3", 2, [140]),
-    ("ar", 1, 3, 0, [141, 172, 206]),
-    ("ar", 1, 3, 1, [143, 181, 198]),
-    ("sh", 2, [147]),
-    ("ap", 2, 2, [148]),
-    ("az", 3, 0, 0, INNER, [149]),
-    ("ar", 1, 2, 1, [151, 178, 193]),
-    ("fo", 2, 2, 1, [204, 165, 152]),
-    ("fo", 2, 2, 0, [214, 164, 153]),
-    ("fo", 2, 3, 1, [200, 171, 155]),
-    ("az", 3, 0, 1, INNER, [156]),
-    ("ap", 2, 0, [157]),
-    ("ys", 2, 0, [182, 162, 158]),
-    ("fo", 2, 3, 0, [226, 167, 159]),
-    ("ap", 2, 1, [160]),
-    ("ys", 2, 1, [190, 168, 161]),
-    ("az", 3, 1, 0, INNER, [166]),
-    ("fo", 2, 0, 0, [245, 192, 169]),
-    ("fo", 2, 1, 0, [229, 202, 174]),
-    ("fo", 2, 0, 1, [217, 195, 175]),
-    ("fo", 2, 1, 1, [242, 201, 179]),
-    ("ar", 3, 1, 0, [183, 210, 239]),
-    ("ar", 3, 0, 0, [184, 209, 234]),
-    ("ar", 3, 3, 0, [185, 219, 256]),
-    ("yo", 2, 0, [186]),
-    ("ar", 3, 2, 1, [187, 215, 243]),
-    ("ar", 3, 2, 0, [188, 221, 259]),
-    ("ar", 3, 1, 1, [189, 212, 231]),
-    ("ar", 3, 0, 1, [194, 213, 236]),
-    ("yo", 2, 1, [196]),
-    ("ar", 3, 3, 1, [197, 216, 253]),
-    ("ay", 3, 0, [199]),
-    ("close", 1, [205]),
-    ("meet", 1, [208]),
-    ("yo", 0, 1, [211]),
-    ("m2", 1, [223]),
-    ("m3", 1, [227]),
-    ("sh", 1, [230]),
-    ("ap", 1, 2, [232]),
-    ("fo", 1, 3, 0, [263, 246, 233]),
-    ("fo", 1, 3, 1, [264, 251, 235]),
-    ("ap", 1, 0, [237]),
-    ("ys", 1, 0, [247, 250, 238]),
-    ("fo", 1, 2, 1, [272, 252, 240]),
-    ("fo", 1, 2, 0, [314, 257, 241]),
-    ("ap", 1, 1, [244]),
-    ("ys", 1, 1, [255, 258, 248]),
-    ("yo", 1, 0, [249]),
-    ("fo", 1, 0, 1, [283, 271, 254]),
-    ("close", 3, [260]),
-    ("meet", 3, [261]),
-    ("fo", 1, 0, 0, [285, 270, 262]),
-    ("fo", 1, 1, 1, [294, 276, 265]),
-    ("m2", 3, [266]),
-    ("yo", 1, 1, [267]),
-    ("fo", 1, 1, 0, [288, 275, 268]),
-    ("ca", 2, 3, [269]),
-    ("ca", 0, 3, [273]),
-    ("m3", 3, [274]),
-    ("co", 2, 1, [277]),
-    ("sh", 3, [278]),
-    ("ap", 3, 1, [279]),
-    ("ys", 3, 1, [291, 282, 280]),
-    ("ap", 3, 2, [281]),
-    ("fo", 3, 2, 1, [327, 296, 284]),
-    ("ap", 3, 0, [286]),
-    ("fo", 3, 3, 0, [307, 292, 287]),
-    ("ys", 3, 0, [301, 290, 289]),
-    ("fo", 3, 3, 1, [318, 309, 293]),
-    ("fo", 3, 1, 0, [317, 305, 295]),
-    ("fo", 3, 2, 0, [324, 312, 297]),
-    ("co", 0, 0, [298]),
-    ("co", 0, 2, [299]),
-    ("fo", 3, 1, 1, [319, 313, 300]),
-    ("ca", 1, 3, [302]),
-    ("fo", 3, 0, 0, [320, 311, 303]),
-    ("fo", 3, 0, 1, [323, 315, 304]),
-    ("co", 2, 2, [306]),
-    ("co", 0, 1, [308]),
-    ("yo", 3, 1, [310]),
-    ("co", 2, 0, [316]),
-    ("yo", 3, 0, [321]),
-    ("co", 1, 0, [322]),
-    ("co", 1, 1, [325]),
-    ("ca", 3, 3, [326]),
-    ("co", 3, 1, [328]),
-    ("co", 1, 2, [329]),
-    ("co", 3, 0, [330]),
-    ("co", 3, 2, [331]),
+    ("az", 0, 1, 1, ([0], [9])),
+    ("ay", 0, 2, ([1], [12])),
+    ("ay", 0, 0, ([2], [38])),
+    ("az", 0, 0, 0, ([3], [29])),
+    ("az", 0, 0, 1, ([4], [19])),
+    ("ay", 3, 2, ([5], [26])),
+    ("az", 0, 1, 0, ([6], [5])),
+    ("az", 0, 2, 1, ([7], [8])),
+    ("az", 2, 0, 0, ([8], [92])),
+    ("az", 3, 1, 0, ([11], [153])),
+    ("ay", 1, 2, ([12], [15])),
+    ("az", 1, 0, 0, ([13], [48])),
+    ("ay", 2, 2, ([14], [21])),
+    ("az", 1, 0, 1, ([15], [24])),
+    ("ar", 0, 1, 1, ([16, 38, 43], [30, 42, 10])),
+    ("ar", 0, 0, 0, ([17, 39, 49], [41, 49, 11])),
+    ("az", 2, 2, 1, ([18], [136])),
+    ("az", 2, 0, 1, ([19], [89])),
+    ("ew", 1, 2, ([20], [56])),
+    ("az", 3, 1, 1, ([21], [150])),
+    ("ew", 0, 2, ([22], [35])),
+    ("ay", 0, 1, ([23], [25])),
+    ("az", 0, 2, 0, ([24], [34])),
+    ("ar", 0, 2, 1, ([25, 60, 81], [51, 67, 68])),
+    ("af", 0, 1, 1, ([26, 53, 45], [36, 63, 372])),
+    ("ar", 0, 1, 0, ([27, 30, 46], [31, 46, 47])),
+    ("az", 0, 3, 1, ([28], [40])),
+    ("az", 0, 3, 0, ([29], [39])),
+    ("az", 1, 1, 0, ([31], [18])),
+    ("az", 1, 1, 1, ([32], [44])),
+    ("af", 0, 1, 0, ([33, 37, 47], [50, 54, 229])),
+    ("ar", 0, 0, 1, ([52, 34, 54], [33, 57, 84])),
+    ("az", 1, 3, 1, ([35], [85])),
+    ("af", 0, 0, 1, ([64, 36, 59], [43, 58, 269])),
+    ("ew", 3, 2, ([40], [88])),
+    ("ar", 0, 3, 0, ([41, 74, 65], [59, 61, 0])),
+    ("af", 0, 0, 0, ([56, 42, 58], [45, 53, 223])),
+    ("az", 1, 3, 0, ([44], [72])),
+    ("az", 2, 2, 0, ([48], [116])),
+    ("ar", 1, 1, 0, ([50, 83, 90], [66, 62, 3])),
+    ("ar", 1, 0, 1, ([51, 76, 86], [60, 80, 37])),
+    ("az", 2, 1, 1, ([55], [105])),
+    ("az", 1, 2, 1, ([57], [91])),
+    ("az", 3, 2, 1, ([61], [184])),
+    ("ar", 1, 0, 0, ([62, 92, 112], [71, 90, 52])),
+    ("cl", 0, 1, ([63], [104])),
+    ("az", 1, 2, 0, ([66], [75])),
+    ("ay", 1, 0, ([67], [108])),
+    ("af", 1, 1, 0, ([68, 119, 106], [77, 76, 28])),
+    ("ar", 0, 3, 1, ([73, 69, 80], [65, 74, 1])),
+    ("mp", 0, 1, ([70], [117])),
+    ("az", 3, 3, 1, ([71], [172])),
+    ("ar", 0, 2, 0, ([72, 82, 75], [64, 55, 2])),
+    ("az", 3, 0, 0, ([77], [125])),
+    ("ar", 1, 1, 1, ([78, 95, 101], [70, 82, 13])),
+    ("af", 1, 0, 0, ([79, 98, 117], [119, 95, 355])),
+    ("az", 3, 2, 0, ([84], [193])),
+    ("mp", 0, 2, ([85], [100])),
+    ("cl", 0, 0, ([87], [102])),
+    ("af", 1, 0, 1, ([94, 88, 96], [81, 110, 366])),
+    ("ay", 3, 1, ([89], [123])),
+    ("ew", 2, 2, ([91], [87])),
+    ("az", 3, 0, 1, ([93], [139])),
+    ("mp", 0, 0, ([97], [106])),
+    ("ay", 2, 0, ([99], [17])),
+    ("az", 2, 1, 0, ([100], [109])),
+    ("az", 3, 3, 0, ([102], [192])),
+    ("meet", 0, ([103], [128])),
+    ("ay", 1, 1, ([104], [73])),
+    ("m2", 0, ([105], [138])),
+    ("az", 2, 3, 0, ([107], [122])),
+    ("ay", 2, 1, ([108], [126])),
+    ("m3", 0, ([109], [149])),
+    ("az", 2, 3, 1, ([110], [133])),
+    ("af", 1, 1, 1, ([111, 114, 113], [83, 96, 239])),
+    ("sh", 0, ([115], [157])),
+    ("ap", 0, 2, ([116], [164])),
+    ("fo", 0, 2, 0, ([118, 130, 144], [254, 218, 382])),
+    ("ar", 1, 3, 0, ([128, 120, 154], [86, 113, 101])),
+    ("fo", 0, 3, 1, ([140, 121, 131], [257, 173, 376])),
+    ("ar", 2, 0, 0, ([122, 133, 189], [99, 134, 4])),
+    ("ay", 3, 0, ([123], [219])),
+    ("fo", 0, 2, 1, ([126, 160, 124], [268, 231, 368])),
+    ("ar", 1, 3, 1, ([143, 125, 158], [97, 124, 127])),
+    ("ar", 2, 0, 1, ([127, 145, 191], [112, 132, 14])),
+    ("ap", 0, 0, ([129], [159])),
+    ("fo", 0, 3, 0, ([146, 172, 132], [258, 220, 166])),
+    ("ys", 0, 0, ([134, 138, 148], [187, 174, 188])),
+    ("ap", 0, 1, ([136], [171])),
+    ("ys", 0, 1, ([193, 137, 161], [246, 189, 190])),
+    ("ar", 1, 2, 1, ([152, 139, 153], [93, 120, 7])),
+    ("cl", 1, 0, ([141], [142])),
+    ("ar", 2, 1, 0, ([142, 183, 185], [118, 144, 16])),
+    ("mp", 1, 0, ([147], [143])),
+    ("ar", 2, 1, 1, ([164, 149, 180], [115, 135, 131])),
+    ("cl", 1, 1, ([150], [130])),
+    ("ar", 1, 2, 0, ([151, 159, 156], [98, 107, 94])),
+    ("af", 2, 1, 0, ([155, 205, 203], [121, 161, 32])),
+    ("mp", 1, 1, ([157], [137])),
+    ("mp", 1, 2, ([162], [129])),
+    ("yo", 0, 1, ([165], [179])),
+    ("fo", 0, 0, 1, ([170, 166, 184], [289, 232, 263])),
+    ("af", 2, 0, 1, ([167, 168, 195], [158, 160, 197])),
+    ("meet", 1, ([169], [148])),
+    ("fo", 0, 1, 0, ([226, 171, 200], [270, 245, 390])),
+    ("ar", 2, 2, 0, ([173, 230, 240], [167, 175, 27])),
+    ("af", 2, 0, 0, ([175, 174, 190], [156, 141, 20])),
+    ("fo", 0, 0, 0, ([194, 176, 182], [303, 272, 394])),
+    ("m2", 1, ([177], [152])),
+    ("yo", 0, 0, ([178], [177])),
+    ("ar", 2, 3, 0, ([179, 227, 225], [147, 163, 78])),
+    ("fo", 0, 1, 1, ([288, 181, 187], [283, 255, 337])),
+    ("m3", 1, ([186], [168])),
+    ("af", 2, 1, 1, ([197, 209, 188], [140, 146, 354])),
+    ("sh", 1, ([192], [176])),
+    ("ap", 1, 2, ([196], [215])),
+    ("ar", 2, 2, 1, ([198, 214, 234], [145, 162, 114])),
+    ("fo", 1, 2, 1, ([236, 220, 199], [286, 227, 224])),
+    ("fo", 1, 3, 1, ([228, 263, 201], [281, 236, 237])),
+    ("fo", 1, 3, 0, ([237, 202, 207], [264, 253, 293])),
+    ("ap", 1, 1, ([204], [183])),
+    ("ar", 3, 0, 0, ([219, 206, 258], [154, 191, 204])),
+    ("fo", 1, 2, 0, ([261, 222, 208], [261, 243, 248])),
+    ("ap", 1, 0, ([211], [180])),
+    ("ys", 1, 0, ([216, 223, 212], [214, 200, 386])),
+    ("ar", 2, 3, 1, ([213, 221, 239], [151, 169, 185])),
+    ("ys", 1, 1, ([250, 232, 215], [251, 216, 325])),
+    ("ar", 3, 1, 0, ([217, 266, 277], [182, 205, 23])),
+    ("cl", 2, 0, ([218], [194])),
+    ("mp", 2, 0, ([224], [195])),
+    ("cl", 2, 1, ([229], [181])),
+    ("mp", 2, 1, ([231], [201])),
+    ("yo", 1, 0, ([233], [300])),
+    ("af", 3, 0, 0, ([251, 235, 260], [230, 213, 217])),
+    ("ar", 3, 1, 1, ([249, 238, 272], [165, 198, 79])),
+    ("mp", 2, 2, ([241], [202])),
+    ("af", 3, 1, 1, ([282, 242, 280], [225, 222, 349])),
+    ("meet", 2, ([243], [210])),
+    ("fo", 1, 0, 1, ([244, 256, 257], [301, 284, 359])),
+    ("ar", 3, 0, 1, ([245, 246, 268], [170, 199, 266])),
+    ("fo", 1, 1, 0, ([281, 310, 247], [311, 282, 379])),
+    ("yo", 1, 1, ([248], [252])),
+    ("ar", 3, 3, 1, ([252, 314, 312], [209, 228, 69])),
+    ("m2", 2, ([253], [226])),
+    ("af", 3, 0, 1, ([254, 262, 269], [203, 241, 297])),
+    ("fo", 1, 1, 1, ([338, 328, 255], [315, 265, 206])),
+    ("fo", 1, 0, 0, ([264, 321, 259], [330, 308, 233])),
+    ("ar", 3, 2, 1, ([265, 295, 316], [221, 256, 155])),
+    ("m3", 2, ([267], [234])),
+    ("af", 3, 1, 0, ([274, 270, 279], [186, 247, 393])),
+    ("sh", 2, ([271], [235])),
+    ("ap", 2, 2, ([273], [262])),
+    ("fo", 2, 2, 0, ([320, 291, 276], [348, 296, 267])),
+    ("fo", 2, 2, 1, ([375, 299, 278], [312, 292, 277])),
+    ("ap", 2, 0, ([283], [240])),
+    ("fo", 2, 3, 0, ([302, 298, 285], [317, 290, 309])),
+    ("fo", 2, 3, 1, ([286, 290, 292], [320, 304, 341])),
+    ("ar", 3, 2, 0, ([287, 293, 308], [211, 238, 244])),
+    ("ys", 2, 0, ([305, 313, 289], [260, 273, 242])),
+    ("ap", 2, 1, ([294], [274])),
+    ("ar", 3, 3, 0, ([296, 304, 317], [208, 249, 212])),
+    ("ys", 2, 1, ([329, 301, 297], [295, 294, 302])),
+    ("cl", 3, 0, ([300], [271])),
+    ("mp", 3, 0, ([303], [285])),
+    ("cl", 3, 1, ([306], [275])),
+    ("mp", 3, 1, ([307], [276])),
+    ("yo", 2, 0, ([309], [278])),
+    ("yo", 2, 1, ([315], [298])),
+    ("mp", 3, 2, ([318], [259])),
+    ("meet", 3, ([319], [288])),
+    ("fo", 2, 1, 1, ([347, 332, 322], [335, 310, 280])),
+    ("fo", 2, 0, 1, ([333, 344, 323], [327, 307, 345])),
+    ("m2", 3, ([324], [291])),
+    ("ca", 0, 3, ([325], [287])),
+    ("fo", 2, 1, 0, ([372, 331, 326], [332, 322, 279])),
+    ("fo", 2, 0, 0, ([378, 350, 327], [334, 329, 362])),
+    ("m3", 3, ([330], [299])),
+    ("sh", 3, ([334], [305])),
+    ("ap", 3, 1, ([335], [313])),
+    ("ys", 3, 1, ([359, 349, 336], [321, 318, 384])),
+    ("ap", 3, 2, ([339], [328])),
+    ("ap", 3, 0, ([341], [306])),
+    ("fo", 3, 3, 1, ([371, 358, 342], [357, 331, 383])),
+    ("ys", 3, 0, ([363, 352, 343], [323, 316, 375])),
+    ("fo", 3, 2, 1, ([389, 366, 345], [369, 353, 395])),
+    ("fo", 3, 3, 0, ([346, 362, 355], [356, 333, 389])),
+    ("fo", 3, 2, 0, ([391, 377, 351], [367, 352, 380])),
+    ("fo", 3, 1, 1, ([374, 369, 353], [360, 346, 370])),
+    ("co", 0, 0, ([354], [347])),
+    ("fo", 3, 1, 0, ([381, 364, 356], [358, 339, 338])),
+    ("fo", 3, 0, 1, ([383, 370, 357], [363, 350, 378])),
+    ("fo", 3, 0, 0, ([382, 365, 360], [361, 343, 344])),
+    ("ca", 2, 3, ([361], [336])),
+    ("ca", 1, 3, ([367], [326])),
+    ("yo", 3, 0, ([368], [365])),
+    ("co", 1, 1, ([373], [351])),
+    ("co", 2, 0, ([376], [371])),
+    ("co", 1, 0, ([379], [381])),
+    ("yo", 3, 1, ([380], [342])),
+    ("co", 0, 2, ([384], [340])),
+    ("ca", 3, 3, ([385], [373])),
+    ("co", 0, 1, ([386], [319])),
+    ("co", 2, 1, ([387], [364])),
+    ("co", 1, 2, ([388], [374])),
+    ("co", 2, 2, ([390], [387])),
+    ("co", 3, 0, ([392], [388])),
+    ("co", 3, 1, ([394], [385])),
+    ("co", 3, 2, ([395], [391])),
 ]
 
 
-def order_of(length):
-    keyed = []
-    for name, group, *rest, slots in SLOTS:
-        if len(slots) == 1:
-            keyed.append((slots[0], (name, group, *rest)))
-            continue
-        for delta in range(1, length):
-            at = (delta - 1) * (len(slots) - 1) / max(length - 2, 1)
-            low = min(int(at), len(slots) - 2)
-            key = slots[low] + (at - low) * (slots[low + 1] - slots[low])
-            keyed.append((key, (name, group, delta, *rest)))
-    return [step for _, step in sorted(keyed, key=lambda pair: pair[0])]
-
-
-def kernel(length, bands, gather_plan, scatter_plan, steps, wave, proj, table, index, count, out,
-           gath, full, term, ysend, yrecv, slot, inter, swap, parts, mixes, weights, own_sem, wave_sem,
-           proj_sem, mix_sem, az_s, az_r, ay_s, ay_r, rz_s, rz_r, ry_s, ry_r, swap_sem, part_s,
-           part_r, wt_sem, out_sem, out_local):
+def waits_of(step, length, gather_plan, scatter_plan):
+    name, g, *rest = step
+    chunks, flows = gather_plan[g], flows_of(gather_plan[g])
+    sums, moves = scatter_plan[g], flows_of(scatter_plan[g])
+    steps = range(1, length)
+    if name == "az" and flows[rest[0]][1]:
+        return [("ew", g, flows[rest[0]][0])]
+    if name == "ew":
+        return [("ay", g, *rest)]
+    if name == "ar":
+        delta, f, d = rest
+        return [("ar", g, delta - 1, f, d) if delta > 1 else ("az", g, f, d)]
+    if name == "af":
+        return [("ar", g, *rest)]
+    if name in ("cl", "mp"):
+        c, = rest
+        single = chunks[c][2]
+        last = "af" if name == "cl" else "ar"
+        waits = [(last, g, delta, f, d) for delta in steps for f, (on, _) in enumerate(flows)
+                 if on == c for d in range(2)]
+        if name == "cl":
+            return waits + [("ay", g, c)]
+        return waits + [("cl" if single else "ew", g, c)]
+    if name == "meet":
+        return [("mp", g, c) for c in range(len(chunks))]
+    before = dict(m2="meet", m3="m2", sh="m3", ap="sh")
+    if name in before:
+        return [(before[name], g)]
+    if name in ("ys", "yo"):
+        return [("ap", g, rest[-1])]
+    if name == "fo":
+        delta, f, d = rest
+        c, _ = moves[f]
+        waits = [("ap", g, c)] + ([("ys", g, delta, c)] if sums[c][2] else [])
+        return waits + ([("fo", g, delta + 1, f, d)] if delta + 1 < length else [])
+    if name in ("ca", "co"):
+        f, = rest
+        c, lane = moves[f]
+        waits = [("ap", g, c), ("fo", g, 1, f, 0), ("fo", g, 1, f, 1)]
+        if not lane:
+            waits.append(("yo", g, c) if sums[c][2] else ("ca", g, moves.index((c, 1))))
+        return waits
+    return []
+
+
+def orders_of(length, gather_plan, scatter_plan):
+    tuned = max(len(slots[0]) for *_, slots in SLOTS) == length - 1
+    orders = []
+    for which in range(2):
+        key = {}
+        for name, group, *rest, slots in SLOTS:
+            slots = slots[which if tuned else 0]
+            if name not in ("ar", "af", "ys", "fo"):
+                key[name, group, *rest] = slots[0]
+                continue
+            for delta in range(1, length):
+                at = (delta - 1) * (len(slots) - 1) / max(length - 2, 1)
+                low = min(int(at), len(slots) - 2)
+                key[name, group, delta, *rest] = (
+                    slots[low] + (at - low) * (slots[low + 1] - slots[low]))
+        if not tuned:
+            moved = True
+            while moved:
+                moved = False
+                for step in key:
+                    for wait in waits_of(step, length, gather_plan, scatter_plan):
+                        if key[step] <= key[wait]:
+                            key[step] = key[wait] + 1e-3
+                            moved = True
+        orders.append(sorted(key, key=key.get))
+    return orders
+
+
+def kernel(length, bands, gather_plan, scatter_plan, steps, wave, proj, table_in, index_in,
+           count_in, out, gath, full, term, ysend, yrecv, slot, inter, swap, parts, mixes, weights,
+           table, index, count, small_sem, own_sem, wave_sem, proj_sem, mix_sem, az_s, az_r, ay_s,
+           ay_r, rz_s, rz_r, ry_s, ry_r, swap_sem, part_s, part_r, wt_sem, out_sem, out_local):
     atom = lax.axis_index("atom")
     band = lax.axis_index("band")
     core = lax.rem(atom, 2)
@@ -297,6 +371,20 @@
     can = (z < length - 1, z > 0)
     edge = (z == 0, z == length - 1)
     partners = [(atom, lax.rem(band + k, bands)) for k in range(1, bands)]
+
+    def span(side, start, size):
+        return pl.ds(pl.multiple_of(side * width + start, 128), size)
+
+    own_copies = []
+    for sub in range(groups // 2):
+        c = pltpu.make_async_copy(wave.at[pl.ds(sub * rows, rows), span(core, 0, width)],
+                                  gath.at[2 * sub + core, 0, z], own_sem.at[sub])
+        c.start()
+        own_copies.append(c)
+    small = [pltpu.make_async_copy(src, dst, small_sem.at[i]) for i, (src, dst) in enumerate(
+        ((table_in, table), (index_in, index), (count_in, count)))]
+    for copy in small:
+        copy.start()
 
     barrier = pltpu.get_barrier_semaphore()
     for target in [peer, across] + partners:
@@ -313,23 +401,24 @@
             src_ref=src, dst_ref=dst, send_sem=s_sem, recv_sem=r_sem,
             device_id=target, device_id_type=MESH)
 
-    def span(side, start, size):
-        return pl.ds(pl.multiple_of(side * width + start, 128), size)
-
-    own_copies, peer_out, peer_in = [], [], []
+    own_out = []
     for sub in range(groups // 2):
-        here = pl.ds(sub * rows, rows)
-        c = remote(wave.at[here, span(other, 0, width)], gath.at[2 * sub + core, 0, z],
-                   wave_sem.at[0, sub], wave_sem.at[1, sub], peer)
+        c = remote(wave.at[pl.ds(sub * rows, rows), span(other, 0, width)],
+                   gath.at[2 * sub + core, 0, z], wave_sem.at[0, sub], wave_sem.at[1, sub], peer)
         c.start()
-        peer_out.append(c)
-        c = pltpu.make_async_copy(wave.at[here, span(core, 0, width)],
-                                  gath.at[2 * sub + core, 0, z], own_sem.at[sub])
-        c.start()
-        own_copies.append(c)
-        peer_in.append(remote(wave.at[here, span(other, 0, width)],
-                              gath.at[2 * sub + other, 0, z],
-                              wave_sem.at[0, sub], wave_sem.at[1, sub], peer))
+        own_out.append(c)
+
+    def entered(g):
+        sub = g // 2
+
+        @pl.when(core == g % 2)
+        def _():
+            own_copies[sub].wait()
+
+        @pl.when(core != g % 2)
+        def _():
+            remote(wave.at[pl.ds(sub * rows, rows), span(other, 0, width)], gath.at[g, 0, z],
+                   wave_sem.at[0, sub], wave_sem.at[1, sub], peer).wait_recv()
 
     gather_flows = [flows_of(p) for p in gather_plan]
     scatter_flows = [flows_of(p) for p in scatter_plan]
@@ -351,14 +440,8 @@
     def start_across(g, c):
         a_y(g, c, z).start()
 
-    def start_along(g, f, d, part):
-        when = can[d]
-        if part == EDGE:
-            when = when & edge[d]
-        if part == INNER:
-            when = when & jnp.logical_not(edge[d])
-
-        @pl.when(when)
+    def start_along(g, f, d):
+        @pl.when(can[d])
         def _():
             a_z(g, f, z, d, True).start()
 
@@ -366,7 +449,6 @@
         a_y(g, c, z).wait_recv()
 
     def arrive(g, delta, f, d):
-        c, _ = gather_flows[g][f]
         block = z - delta if d == 0 else z + delta
 
         @pl.when(block >= 0 if d == 0 else block < length)
@@ -377,32 +459,41 @@
             @pl.when(can[d])
             def _():
                 copy.start()
-            if gather_plan[g][c][2]:
-                a_y(g, c, block).start()
-
-    def gather_close(g):
-        for c, chunk in enumerate(gather_plan[g]):
-            if chunk[2]:
-                for block in range(length):
-                    a_y(g, c, block).wait_recv()
-
-    kt = min(1024, width)
+
+    def arrived_across(g, delta, f, d):
+        c, _ = gather_flows[g][f]
+        block = z - delta if d == 0 else z + delta
+
+        @pl.when(block >= 0 if d == 0 else block < length)
+        def _():
+            a_y(g, c, block).start()
+
+    def gather_close(g, c):
+        for block in range(length):
+            a_y(g, c, block).wait_recv()
+
     keep, give = core, other
-
-    def meet(g):
-        if g == 0:
-            proj_local.wait()
-            proj_in.wait_recv()
-            mix_in.wait_recv()
+    met = set()
+
+    def meet(g, c):
+        start, size, _ = gather_plan[g][c]
+        kt = next(unit * n for n in (2, 1) if size % (unit * n) == 0)
 
         def body(t, acc):
-            where = pl.ds(pl.multiple_of(t * kt, kt), kt)
+            where = pl.ds(pl.multiple_of(start + t * kt, unit), kt)
             left = gath[g, :, :, :, where].reshape(2 * half_rows, kt)
             return acc + lax.dot_general(left, full[:, where], (((1,), (1,)), ((), ())),
                                          preferred_element_type=jnp.float32)
 
-        total = lax.fori_loop(0, width // kt, body, jnp.zeros((2 * half_rows, both), jnp.float32))
+        if g in met:
+            total = inter[g].reshape(2 * half_rows, both)
+        else:
+            total = jnp.zeros((2 * half_rows, both), jnp.float32)
+        met.add(g)
+        total = lax.fori_loop(0, size // kt, body, total)
         inter[g] = total.reshape(2, half_rows, both)
+
+    def met_all(g):
         core_sum(g).start()
 
     def core_sum(g):
@@ -572,14 +663,10 @@
         def _():
             far.start()
 
-    def entered(sub):
-        own_copies[sub].wait()
-        peer_in[sub].wait_recv()
-
     run = dict(
-        ay=start_across, az=start_along, ew=enter, ar=arrive, close=gather_close, meet=meet,
-        m2=middle_two, m3=middle_three, sh=shared, ap=apply, ys=send_across,
-        yo=send_own_across, fo=fold, ca=collect_across, co=collect_own)
+        ay=start_across, az=start_along, ew=enter, ar=arrive, af=arrived_across, cl=gather_close,
+        mp=meet, meet=met_all, m2=middle_two, m3=middle_three, sh=shared, ap=apply,
+        ys=send_across, yo=send_own_across, fo=fold, ca=collect_across, co=collect_own)
     mine = pl.ds(pl.multiple_of(core * depth, depth), depth)
     theirs = pl.ds(pl.multiple_of(other * depth, depth), depth)
     proj_local = pltpu.make_async_copy(proj.at[:, span(core, 0, width)], full.at[mine, :],
@@ -594,22 +681,41 @@
     def prepare():
         proj_local.start()
         proj_out.start()
-        mixes[core] = mix_matrix(table, index[...], count[...])
+        for copy in small:
+            copy.wait()
+        mixes[core] = mix_matrix(table, index, count)
         mix_out.start()
 
-    inside, prepared = set(), False
-    for name, g, *rest in steps:
-        if name in ("ay", "az"):
-            if g // 2 not in inside:
-                entered(g // 2)
-                inside.add(g // 2)
-        elif not prepared:
-            prepare()
-            prepared = True
-        run[name](g, *rest)
-
-    for sub in range(groups // 2):
-        peer_out[sub].wait_send()
+    def play(steps):
+        met.clear()
+        prepared = ready = False
+        inside = set()
+        for name, *rest in steps:
+            if name in ("ay", "az") and rest[0] not in inside:
+                entered(rest[0])
+                inside.add(rest[0])
+            if not prepared and name not in ("ay", "az"):
+                prepare()
+                prepared = True
+            if not ready and name == "mp":
+                proj_local.wait()
+                proj_in.wait_recv()
+                mix_in.wait_recv()
+                ready = True
+            run[name](*rest)
+
+    at_end = edge[0] | edge[1]
+
+    @pl.when(at_end)
+    def _():
+        play(steps[0])
+
+    @pl.when(jnp.logical_not(at_end))
+    def _():
+        play(steps[1])
+
+    for c in own_out:
+        c.wait_send()
     proj_out.wait_send()
     mix_out.wait_send()
     for g in range(groups):
@@ -671,7 +777,7 @@
     others = max(bands - 1, 1)
     gather_plan = [chunks_of(width, share) for share in GATHER_SHARE]
     scatter_plan = [chunks_of(width, share) for share in SCATTER_SHARE]
-    steps = order_of(length)
+    steps = orders_of(length, gather_plan, scatter_plan)
     chunks = max(len(p) for p in gather_plan + scatter_plan)
     flows = max(len(flows_of(p)) for p in gather_plan + scatter_plan)
     dma = pltpu.SemaphoreType.DMA
@@ -680,7 +786,7 @@
     return pl.pallas_call(
         functools.partial(kernel, length, bands, gather_plan, scatter_plan, steps),
         out_shape=jax.ShapeDtypeStruct((all_rows, columns), bf16),
-        in_specs=[anywhere, anywhere] + [pl.BlockSpec(memory_space=pltpu.VMEM)] * 3,
+        in_specs=[anywhere] * 5,
         out_specs=anywhere,
         scratch_shapes=[
             pltpu.VMEM((groups, 2, length, rows, width), bf16),
@@ -694,7 +800,9 @@
             pltpu.VMEM((groups, others, length * rows, both), f32),
             pltpu.VMEM((2, depth, depth), f32),
             pltpu.VMEM((groups, 2, length * rows, both), bf16),
-            dma((groups // 2 + 1,)), dma((2, groups // 2)), dma((2,)), dma((2,)),
+            pltpu.VMEM(dij_table.shape[1:] + dij_table.shape[:1], f32),
+            pltpu.SMEM(dij_index.shape, jnp.int32), pltpu.SMEM(proj_count.shape, jnp.int32),
+            dma((3,)), dma((groups // 2 + 1,)), dma((2, groups // 2)), dma((2,)), dma((2,)),
             dma((groups, flows, length + 1)), dma((groups, flows, length)),
             dma((groups, chunks, length)), dma((groups, chunks, length)),
             dma((groups, flows, length)), dma((groups, flows, length + 1)),
@@ -705,7 +813,7 @@
         compiler_params=pltpu.CompilerParams(
             collective_id=0, has_side_effects=True, vmem_limit_bytes=60 * 1024 * 1024
         ),
-    )(wave_rows, projectors, dij_table, dij_index[:, None], proj_count[:, None])
+    )(wave_rows, projectors, jnp.transpose(dij_table, (1, 2, 0)), dij_index, proj_count)
 
 
 def solution(mesh):

time: 160 us -> 147 us (0.919)
  Pallas kernels: 152 us -> 145 us
  local copies, waits for them, and re-layouts: 6.38 us -> 2.26 us
    pallas_call x1, Pallas kernels: 152 us -> 145 us  [shards(): pl.pallas_call(functools.partial(kernel, length, bands, gather_plan, scat...]
    broadcast_in_dim x2 -> x0, local copies, waits for them, and re-layouts: 2.65 us -> none  [the longest x1 1.33 us: shards(): proj_count[:, None]]
    unnamed x2 -> x1, local copies, waits for them, and re-layouts: 3.73 us -> 2.26 us
where the time goes in v3:
time: 147 us
  Pallas kernels  145 us (99%)
  local copies, waits for them, and re-layouts  2.26 us (2%)
    pallas_call x1, Pallas kernels, shards(): pl.pallas_call(functools.partial(kernel, length, bands, gather_plan, scat...  145 us

profile of v3, /device:TPU:0, one launch (start us, length us, event | category | flops | bytes accessed | tf_op | source)
XLA Modules:
  0.0 146.8 jit_solution(236825405126328916)
XLA Ops:
  0.0 144.6 %shard_map.68 = bf16[16,32768]{1,0:T(8,128)(2,1)} custom-call(bf16[16,32768]{1,0:T(8,128)(2,1)} %wave.1, bf16[128,32768]{1,0:T(8,128)(2,1)} %proj.1, f32[8,8,16]{2,1,0:T(8,128)} %bitcast.1, s32[16]{0:T(128)} %index_in.1, s32[16]{0:T(128)} %count_in.1), custom_call_target="tpu_custom_call" | custom-call | tf_op jit(solution)/jit(shards)/shard_map/pallas_call | solution.py:786
  144.6 2.3 %copy.7 = bf16[16,32768]{1,0:T(8,128)(2,1)} copy(bf16[16,32768]{1,0:T(8,128)(2,1)} %shard_map.68) | data formatting | bytes 2097152

commit v4 on v3

--- a/solution.py
+++ b/solution.py
@@ -9,8 +9,8 @@
 
 MESH = pl.DeviceIdType.MESH
 GROUPS = 4
-GATHER_SHARE = (0.875, 0.625, 0.5625, 0.5)
-SCATTER_SHARE = (0.5, 0.5625, 0.625, 0.875)
+GATHER_SHARE = (0.84375, 0.59375, 0.53125, 0.5)
+SCATTER_SHARE = (0.5, 0.53125, 0.59375, 0.84375)
 PARTS = (2, 1)
 
 
@@ -61,214 +61,214 @@
 
 
 SLOTS = [
-    ("az", 0, 1, 1, ([0], [9])),
-    ("ay", 0, 2, ([1], [12])),
-    ("ay", 0, 0, ([2], [38])),
-    ("az", 0, 0, 0, ([3], [29])),
-    ("az", 0, 0, 1, ([4], [19])),
-    ("ay", 3, 2, ([5], [26])),
-    ("az", 0, 1, 0, ([6], [5])),
-    ("az", 0, 2, 1, ([7], [8])),
-    ("az", 2, 0, 0, ([8], [92])),
-    ("az", 3, 1, 0, ([11], [153])),
-    ("ay", 1, 2, ([12], [15])),
-    ("az", 1, 0, 0, ([13], [48])),
-    ("ay", 2, 2, ([14], [21])),
-    ("az", 1, 0, 1, ([15], [24])),
-    ("ar", 0, 1, 1, ([16, 38, 43], [30, 42, 10])),
-    ("ar", 0, 0, 0, ([17, 39, 49], [41, 49, 11])),
-    ("az", 2, 2, 1, ([18], [136])),
-    ("az", 2, 0, 1, ([19], [89])),
-    ("ew", 1, 2, ([20], [56])),
-    ("az", 3, 1, 1, ([21], [150])),
-    ("ew", 0, 2, ([22], [35])),
-    ("ay", 0, 1, ([23], [25])),
-    ("az", 0, 2, 0, ([24], [34])),
-    ("ar", 0, 2, 1, ([25, 60, 81], [51, 67, 68])),
-    ("af", 0, 1, 1, ([26, 53, 45], [36, 63, 372])),
-    ("ar", 0, 1, 0, ([27, 30, 46], [31, 46, 47])),
-    ("az", 0, 3, 1, ([28], [40])),
-    ("az", 0, 3, 0, ([29], [39])),
-    ("az", 1, 1, 0, ([31], [18])),
-    ("az", 1, 1, 1, ([32], [44])),
-    ("af", 0, 1, 0, ([33, 37, 47], [50, 54, 229])),
-    ("ar", 0, 0, 1, ([52, 34, 54], [33, 57, 84])),
-    ("az", 1, 3, 1, ([35], [85])),
-    ("af", 0, 0, 1, ([64, 36, 59], [43, 58, 269])),
-    ("ew", 3, 2, ([40], [88])),
-    ("ar", 0, 3, 0, ([41, 74, 65], [59, 61, 0])),
-    ("af", 0, 0, 0, ([56, 42, 58], [45, 53, 223])),
-    ("az", 1, 3, 0, ([44], [72])),
-    ("az", 2, 2, 0, ([48], [116])),
-    ("ar", 1, 1, 0, ([50, 83, 90], [66, 62, 3])),
-    ("ar", 1, 0, 1, ([51, 76, 86], [60, 80, 37])),
-    ("az", 2, 1, 1, ([55], [105])),
-    ("az", 1, 2, 1, ([57], [91])),
-    ("az", 3, 2, 1, ([61], [184])),
-    ("ar", 1, 0, 0, ([62, 92, 112], [71, 90, 52])),
-    ("cl", 0, 1, ([63], [104])),
-    ("az", 1, 2, 0, ([66], [75])),
-    ("ay", 1, 0, ([67], [108])),
-    ("af", 1, 1, 0, ([68, 119, 106], [77, 76, 28])),
-    ("ar", 0, 3, 1, ([73, 69, 80], [65, 74, 1])),
-    ("mp", 0, 1, ([70], [117])),
-    ("az", 3, 3, 1, ([71], [172])),
-    ("ar", 0, 2, 0, ([72, 82, 75], [64, 55, 2])),
-    ("az", 3, 0, 0, ([77], [125])),
-    ("ar", 1, 1, 1, ([78, 95, 101], [70, 82, 13])),
-    ("af", 1, 0, 0, ([79, 98, 117], [119, 95, 355])),
-    ("az", 3, 2, 0, ([84], [193])),
-    ("mp", 0, 2, ([85], [100])),
-    ("cl", 0, 0, ([87], [102])),
-    ("af", 1, 0, 1, ([94, 88, 96], [81, 110, 366])),
-    ("ay", 3, 1, ([89], [123])),
-    ("ew", 2, 2, ([91], [87])),
-    ("az", 3, 0, 1, ([93], [139])),
-    ("mp", 0, 0, ([97], [106])),
-    ("ay", 2, 0, ([99], [17])),
-    ("az", 2, 1, 0, ([100], [109])),
-    ("az", 3, 3, 0, ([102], [192])),
-    ("meet", 0, ([103], [128])),
-    ("ay", 1, 1, ([104], [73])),
-    ("m2", 0, ([105], [138])),
-    ("az", 2, 3, 0, ([107], [122])),
-    ("ay", 2, 1, ([108], [126])),
-    ("m3", 0, ([109], [149])),
-    ("az", 2, 3, 1, ([110], [133])),
-    ("af", 1, 1, 1, ([111, 114, 113], [83, 96, 239])),
-    ("sh", 0, ([115], [157])),
-    ("ap", 0, 2, ([116], [164])),
-    ("fo", 0, 2, 0, ([118, 130, 144], [254, 218, 382])),
-    ("ar", 1, 3, 0, ([128, 120, 154], [86, 113, 101])),
-    ("fo", 0, 3, 1, ([140, 121, 131], [257, 173, 376])),
-    ("ar", 2, 0, 0, ([122, 133, 189], [99, 134, 4])),
-    ("ay", 3, 0, ([123], [219])),
-    ("fo", 0, 2, 1, ([126, 160, 124], [268, 231, 368])),
-    ("ar", 1, 3, 1, ([143, 125, 158], [97, 124, 127])),
-    ("ar", 2, 0, 1, ([127, 145, 191], [112, 132, 14])),
-    ("ap", 0, 0, ([129], [159])),
-    ("fo", 0, 3, 0, ([146, 172, 132], [258, 220, 166])),
-    ("ys", 0, 0, ([134, 138, 148], [187, 174, 188])),
-    ("ap", 0, 1, ([136], [171])),
-    ("ys", 0, 1, ([193, 137, 161], [246, 189, 190])),
-    ("ar", 1, 2, 1, ([152, 139, 153], [93, 120, 7])),
-    ("cl", 1, 0, ([141], [142])),
-    ("ar", 2, 1, 0, ([142, 183, 185], [118, 144, 16])),
-    ("mp", 1, 0, ([147], [143])),
-    ("ar", 2, 1, 1, ([164, 149, 180], [115, 135, 131])),
-    ("cl", 1, 1, ([150], [130])),
-    ("ar", 1, 2, 0, ([151, 159, 156], [98, 107, 94])),
-    ("af", 2, 1, 0, ([155, 205, 203], [121, 161, 32])),
-    ("mp", 1, 1, ([157], [137])),
-    ("mp", 1, 2, ([162], [129])),
-    ("yo", 0, 1, ([165], [179])),
-    ("fo", 0, 0, 1, ([170, 166, 184], [289, 232, 263])),
-    ("af", 2, 0, 1, ([167, 168, 195], [158, 160, 197])),
-    ("meet", 1, ([169], [148])),
-    ("fo", 0, 1, 0, ([226, 171, 200], [270, 245, 390])),
-    ("ar", 2, 2, 0, ([173, 230, 240], [167, 175, 27])),
-    ("af", 2, 0, 0, ([175, 174, 190], [156, 141, 20])),
-    ("fo", 0, 0, 0, ([194, 176, 182], [303, 272, 394])),
-    ("m2", 1, ([177], [152])),
-    ("yo", 0, 0, ([178], [177])),
-    ("ar", 2, 3, 0, ([179, 227, 225], [147, 163, 78])),
-    ("fo", 0, 1, 1, ([288, 181, 187], [283, 255, 337])),
-    ("m3", 1, ([186], [168])),
-    ("af", 2, 1, 1, ([197, 209, 188], [140, 146, 354])),
-    ("sh", 1, ([192], [176])),
-    ("ap", 1, 2, ([196], [215])),
-    ("ar", 2, 2, 1, ([198, 214, 234], [145, 162, 114])),
-    ("fo", 1, 2, 1, ([236, 220, 199], [286, 227, 224])),
-    ("fo", 1, 3, 1, ([228, 263, 201], [281, 236, 237])),
-    ("fo", 1, 3, 0, ([237, 202, 207], [264, 253, 293])),
-    ("ap", 1, 1, ([204], [183])),
-    ("ar", 3, 0, 0, ([219, 206, 258], [154, 191, 204])),
-    ("fo", 1, 2, 0, ([261, 222, 208], [261, 243, 248])),
-    ("ap", 1, 0, ([211], [180])),
-    ("ys", 1, 0, ([216, 223, 212], [214, 200, 386])),
-    ("ar", 2, 3, 1, ([213, 221, 239], [151, 169, 185])),
-    ("ys", 1, 1, ([250, 232, 215], [251, 216, 325])),
-    ("ar", 3, 1, 0, ([217, 266, 277], [182, 205, 23])),
-    ("cl", 2, 0, ([218], [194])),
-    ("mp", 2, 0, ([224], [195])),
-    ("cl", 2, 1, ([229], [181])),
-    ("mp", 2, 1, ([231], [201])),
-    ("yo", 1, 0, ([233], [300])),
-    ("af", 3, 0, 0, ([251, 235, 260], [230, 213, 217])),
-    ("ar", 3, 1, 1, ([249, 238, 272], [165, 198, 79])),
-    ("mp", 2, 2, ([241], [202])),
-    ("af", 3, 1, 1, ([282, 242, 280], [225, 222, 349])),
-    ("meet", 2, ([243], [210])),
-    ("fo", 1, 0, 1, ([244, 256, 257], [301, 284, 359])),
-    ("ar", 3, 0, 1, ([245, 246, 268], [170, 199, 266])),
-    ("fo", 1, 1, 0, ([281, 310, 247], [311, 282, 379])),
-    ("yo", 1, 1, ([248], [252])),
-    ("ar", 3, 3, 1, ([252, 314, 312], [209, 228, 69])),
-    ("m2", 2, ([253], [226])),
-    ("af", 3, 0, 1, ([254, 262, 269], [203, 241, 297])),
-    ("fo", 1, 1, 1, ([338, 328, 255], [315, 265, 206])),
-    ("fo", 1, 0, 0, ([264, 321, 259], [330, 308, 233])),
-    ("ar", 3, 2, 1, ([265, 295, 316], [221, 256, 155])),
-    ("m3", 2, ([267], [234])),
-    ("af", 3, 1, 0, ([274, 270, 279], [186, 247, 393])),
-    ("sh", 2, ([271], [235])),
-    ("ap", 2, 2, ([273], [262])),
-    ("fo", 2, 2, 0, ([320, 291, 276], [348, 296, 267])),
-    ("fo", 2, 2, 1, ([375, 299, 278], [312, 292, 277])),
-    ("ap", 2, 0, ([283], [240])),
-    ("fo", 2, 3, 0, ([302, 298, 285], [317, 290, 309])),
-    ("fo", 2, 3, 1, ([286, 290, 292], [320, 304, 341])),
-    ("ar", 3, 2, 0, ([287, 293, 308], [211, 238, 244])),
-    ("ys", 2, 0, ([305, 313, 289], [260, 273, 242])),
-    ("ap", 2, 1, ([294], [274])),
-    ("ar", 3, 3, 0, ([296, 304, 317], [208, 249, 212])),
-    ("ys", 2, 1, ([329, 301, 297], [295, 294, 302])),
-    ("cl", 3, 0, ([300], [271])),
-    ("mp", 3, 0, ([303], [285])),
-    ("cl", 3, 1, ([306], [275])),
-    ("mp", 3, 1, ([307], [276])),
-    ("yo", 2, 0, ([309], [278])),
-    ("yo", 2, 1, ([315], [298])),
-    ("mp", 3, 2, ([318], [259])),
-    ("meet", 3, ([319], [288])),
-    ("fo", 2, 1, 1, ([347, 332, 322], [335, 310, 280])),
-    ("fo", 2, 0, 1, ([333, 344, 323], [327, 307, 345])),
-    ("m2", 3, ([324], [291])),
-    ("ca", 0, 3, ([325], [287])),
-    ("fo", 2, 1, 0, ([372, 331, 326], [332, 322, 279])),
-    ("fo", 2, 0, 0, ([378, 350, 327], [334, 329, 362])),
-    ("m3", 3, ([330], [299])),
-    ("sh", 3, ([334], [305])),
-    ("ap", 3, 1, ([335], [313])),
-    ("ys", 3, 1, ([359, 349, 336], [321, 318, 384])),
-    ("ap", 3, 2, ([339], [328])),
-    ("ap", 3, 0, ([341], [306])),
-    ("fo", 3, 3, 1, ([371, 358, 342], [357, 331, 383])),
-    ("ys", 3, 0, ([363, 352, 343], [323, 316, 375])),
-    ("fo", 3, 2, 1, ([389, 366, 345], [369, 353, 395])),
-    ("fo", 3, 3, 0, ([346, 362, 355], [356, 333, 389])),
-    ("fo", 3, 2, 0, ([391, 377, 351], [367, 352, 380])),
-    ("fo", 3, 1, 1, ([374, 369, 353], [360, 346, 370])),
-    ("co", 0, 0, ([354], [347])),
-    ("fo", 3, 1, 0, ([381, 364, 356], [358, 339, 338])),
-    ("fo", 3, 0, 1, ([383, 370, 357], [363, 350, 378])),
-    ("fo", 3, 0, 0, ([382, 365, 360], [361, 343, 344])),
-    ("ca", 2, 3, ([361], [336])),
-    ("ca", 1, 3, ([367], [326])),
-    ("yo", 3, 0, ([368], [365])),
-    ("co", 1, 1, ([373], [351])),
-    ("co", 2, 0, ([376], [371])),
-    ("co", 1, 0, ([379], [381])),
-    ("yo", 3, 1, ([380], [342])),
-    ("co", 0, 2, ([384], [340])),
-    ("ca", 3, 3, ([385], [373])),
-    ("co", 0, 1, ([386], [319])),
-    ("co", 2, 1, ([387], [364])),
-    ("co", 1, 2, ([388], [374])),
-    ("co", 2, 2, ([390], [387])),
-    ("co", 3, 0, ([392], [388])),
-    ("co", 3, 1, ([394], [385])),
-    ("co", 3, 2, ([395], [391])),
+    ("ay", 0, 2, ([0], [13])),
+    ("ay", 2, 2, ([1], [22])),
+    ("az", 0, 0, 0, ([2], [0])),
+    ("az", 0, 1, 1, ([3], [8])),
+    ("az", 0, 1, 0, ([4], [14])),
+    ("az", 3, 1, 0, ([5], [69])),
+    ("az", 0, 0, 1, ([6], [15])),
+    ("az", 0, 2, 0, ([7], [21])),
+    ("ay", 1, 2, ([8], [73])),
+    ("ar", 0, 0, 0, ([9, 53, 51], [28, 51, 4])),
+    ("ew", 0, 2, ([10], [25])),
+    ("ar", 0, 1, 1, ([11, 21, 38], [20, 33, 32])),
+    ("az", 3, 1, 1, ([12], [148])),
+    ("az", 2, 0, 0, ([13], [19])),
+    ("ay", 0, 0, ([14], [12])),
+    ("az", 1, 2, 0, ([15], [135])),
+    ("af", 0, 1, 1, ([16, 23, 50], [23, 40, 392])),
+    ("ar", 0, 1, 0, ([17, 31, 47], [24, 37, 54])),
+    ("az", 0, 2, 1, ([18], [16])),
+    ("az", 0, 3, 1, ([19], [27])),
+    ("az", 2, 0, 1, ([20], [30])),
+    ("az", 2, 1, 1, ([22], [50])),
+    ("af", 0, 0, 0, ([24, 57, 52], [56, 70, 162])),
+    ("ew", 2, 2, ([25], [65])),
+    ("ar", 0, 2, 1, ([26, 64, 76], [41, 55, 34])),
+    ("az", 0, 3, 0, ([27], [35])),
+    ("az", 2, 1, 0, ([28], [57])),
+    ("ay", 0, 1, ([29], [11])),
+    ("ar", 0, 0, 1, ([30, 36, 59], [26, 46, 60])),
+    ("az", 2, 2, 0, ([32], [88])),
+    ("az", 3, 2, 0, ([33], [204])),
+    ("af", 0, 0, 1, ([34, 58, 63], [59, 47, 268])),
+    ("az", 1, 1, 0, ([35], [110])),
+    ("af", 0, 1, 0, ([44, 37, 48], [31, 48, 97])),
+    ("az", 2, 3, 1, ([39], [76])),
+    ("ar", 2, 0, 0, ([40, 74, 99], [53, 75, 17])),
+    ("az", 2, 2, 1, ([42], [64])),
+    ("az", 1, 2, 1, ([43], [137])),
+    ("az", 3, 2, 1, ([45], [200])),
+    ("az", 2, 3, 0, ([46], [82])),
+    ("ar", 0, 3, 0, ([49, 69, 79], [52, 67, 36])),
+    ("az", 1, 0, 0, ([54], [79])),
+    ("ar", 0, 3, 1, ([55, 60, 81], [49, 58, 39])),
+    ("az", 1, 1, 1, ([61], [86])),
+    ("ar", 0, 2, 0, ([62, 78, 75], [44, 62, 9])),
+    ("az", 1, 0, 1, ([65], [107])),
+    ("ay", 3, 2, ([66], [145])),
+    ("ay", 3, 0, ([67], [198])),
+    ("ew", 1, 2, ([68], [115])),
+    ("ay", 1, 1, ([70], [85])),
+    ("cl", 0, 1, ([71], [71])),
+    ("az", 3, 0, 1, ([72], [122])),
+    ("mp", 0, 1, ([73], [80])),
+    ("af", 2, 0, 0, ([80, 77, 104], [113, 100, 245])),
+    ("mp", 0, 2, ([82], [68])),
+    ("ar", 2, 1, 1, ([83, 100, 116], [72, 84, 116])),
+    ("cl", 0, 0, ([85], [92])),
+    ("mp", 0, 0, ([86], [95])),
+    ("meet", 0, ([87], [99])),
+    ("az", 1, 3, 1, ([88], [141])),
+    ("ar", 2, 1, 0, ([93, 89, 113], [77, 81, 114])),
+    ("az", 3, 0, 0, ([90], [181])),
+    ("ar", 2, 0, 1, ([91, 108, 110], [61, 74, 5])),
+    ("af", 2, 1, 0, ([109, 92, 117], [96, 109, 236])),
+    ("af", 2, 0, 1, ([94, 114, 115], [78, 111, 118])),
+    ("m2", 0, ([95], [102])),
+    ("ay", 2, 0, ([96], [112])),
+    ("ew", 3, 2, ([97], [175])),
+    ("ar", 3, 1, 0, ([98, 276, 259], [184, 193, 254])),
+    ("af", 3, 1, 0, ([102, 288, 261], [232, 233, 266])),
+    ("az", 3, 3, 0, ([103], [202])),
+    ("ay", 1, 0, ([105], [94])),
+    ("az", 3, 3, 1, ([106], [196])),
+    ("ay", 2, 1, ([107], [106])),
+    ("m3", 0, ([111], [123])),
+    ("af", 2, 1, 1, ([112, 121, 118], [108, 89, 253])),
+    ("az", 1, 3, 0, ([119], [127])),
+    ("ar", 2, 3, 1, ([120, 135, 157], [98, 119, 18])),
+    ("sh", 0, ([122], [133])),
+    ("ap", 0, 2, ([123], [159])),
+    ("fo", 0, 3, 1, ([141, 131, 124], [261, 173, 389])),
+    ("fo", 0, 3, 0, ([178, 128, 125], [267, 171, 311])),
+    ("ap", 0, 0, ([126], [165])),
+    ("ar", 2, 2, 1, ([154, 127, 159], [91, 117, 93])),
+    ("fo", 0, 2, 0, ([145, 129, 140], [282, 186, 301])),
+    ("fo", 0, 2, 1, ([151, 155, 130], [281, 176, 328])),
+    ("ys", 0, 0, ([146, 132, 137], [183, 195, 279])),
+    ("ap", 0, 1, ([133], [144])),
+    ("ar", 2, 3, 0, ([148, 134, 156], [101, 121, 63])),
+    ("ar", 2, 2, 0, ([136, 158, 160], [103, 126, 43])),
+    ("ar", 1, 0, 0, ([174, 138, 202], [104, 154, 7])),
+    ("ar", 1, 1, 1, ([139, 170, 179], [120, 131, 1])),
+    ("ys", 0, 1, ([152, 149, 142], [192, 155, 376])),
+    ("cl", 2, 0, ([143], [147])),
+    ("mp", 2, 0, ([144], [149])),
+    ("cl", 2, 1, ([147], [134])),
+    ("mp", 2, 1, ([150], [138])),
+    ("ar", 1, 0, 1, ([153, 184, 193], [124, 140, 132])),
+    ("mp", 2, 2, ([161], [130])),
+    ("meet", 2, ([162], [150])),
+    ("af", 1, 0, 0, ([182, 163, 203], [125, 161, 388])),
+    ("fo", 0, 0, 1, ([186, 164, 176], [299, 246, 260])),
+    ("fo", 0, 0, 0, ([165, 199, 204], [325, 300, 345])),
+    ("yo", 0, 0, ([166], [213])),
+    ("fo", 0, 1, 0, ([173, 181, 167], [296, 211, 168])),
+    ("ar", 1, 1, 0, ([168, 192, 194], [142, 153, 6])),
+    ("ay", 3, 1, ([169], [197])),
+    ("fo", 0, 1, 1, ([188, 171, 196], [332, 275, 384])),
+    ("m2", 2, ([172], [163])),
+    ("ar", 1, 2, 0, ([175, 226, 231], [158, 177, 166])),
+    ("af", 1, 1, 1, ([177, 191, 197], [156, 170, 391])),
+    ("af", 1, 0, 1, ([180, 187, 207], [136, 143, 265])),
+    ("ar", 3, 0, 1, ([183, 249, 281], [179, 215, 3])),
+    ("af", 1, 1, 0, ([185, 195, 200], [146, 167, 128])),
+    ("m3", 2, ([190], [182])),
+    ("ar", 1, 3, 0, ([198, 221, 240], [157, 180, 129])),
+    ("sh", 2, ([205], [191])),
+    ("ap", 2, 2, ([206], [223])),
+    ("fo", 2, 3, 0, ([254, 237, 208], [264, 238, 252])),
+    ("af", 3, 0, 1, ([209, 277, 283], [207, 256, 194])),
+    ("fo", 2, 3, 1, ([215, 230, 210], [257, 231, 368])),
+    ("ap", 2, 0, ([212], [205])),
+    ("ys", 2, 0, ([220, 214, 213], [228, 219, 214])),
+    ("fo", 2, 2, 1, ([243, 244, 216], [272, 227, 284])),
+    ("ap", 2, 1, ([217], [208])),
+    ("fo", 2, 2, 0, ([225, 218, 222], [274, 234, 338])),
+    ("ar", 1, 3, 1, ([224, 219, 234], [151, 169, 105])),
+    ("cl", 1, 1, ([223], [188])),
+    ("ar", 1, 2, 1, ([235, 227, 239], [152, 172, 38])),
+    ("mp", 1, 1, ([228], [199])),
+    ("cl", 1, 0, ([229], [201])),
+    ("mp", 1, 0, ([232], [203])),
+    ("fo", 2, 0, 1, ([267, 245, 233], [331, 304, 393])),
+    ("ys", 2, 1, ([251, 238, 236], [237, 226, 255])),
+    ("mp", 1, 2, ([241], [185])),
+    ("meet", 1, ([242], [206])),
+    ("fo", 2, 0, 0, ([256, 246, 262], [285, 271, 243])),
+    ("fo", 2, 1, 0, ([279, 264, 247], [318, 259, 247])),
+    ("ar", 3, 1, 1, ([269, 271, 248], [174, 190, 10])),
+    ("m2", 1, ([253], [212])),
+    ("fo", 2, 1, 1, ([287, 265, 257], [298, 277, 316])),
+    ("yo", 2, 1, ([258], [287])),
+    ("yo", 2, 0, ([260], [216])),
+    ("ar", 3, 0, 0, ([266, 263, 275], [187, 209, 248])),
+    ("yo", 0, 1, ([268], [242])),
+    ("af", 3, 0, 0, ([270, 278, 282], [229, 210, 288])),
+    ("ar", 3, 3, 1, ([272, 302, 310], [221, 230, 160])),
+    ("ar", 3, 2, 0, ([273, 309, 318], [224, 249, 66])),
+    ("m3", 1, ([274], [225])),
+    ("ar", 3, 3, 0, ([280, 293, 311], [220, 239, 139])),
+    ("ar", 3, 2, 1, ([284, 308, 317], [222, 250, 218])),
+    ("af", 3, 1, 1, ([291, 286, 285], [189, 217, 90])),
+    ("sh", 1, ([289], [235])),
+    ("ap", 1, 2, ([290], [241])),
+    ("fo", 1, 2, 0, ([316, 336, 292], [329, 303, 262])),
+    ("fo", 1, 2, 1, ([324, 298, 294], [306, 286, 290])),
+    ("fo", 1, 3, 1, ([301, 321, 295], [315, 293, 276])),
+    ("ap", 1, 0, ([296], [244])),
+    ("ys", 1, 0, ([323, 322, 297], [263, 307, 258])),
+    ("fo", 1, 3, 0, ([327, 300, 299], [310, 295, 390])),
+    ("ap", 1, 1, ([303], [240])),
+    ("ys", 1, 1, ([314, 304, 306], [292, 270, 382])),
+    ("cl", 3, 0, ([305], [280])),
+    ("mp", 3, 0, ([307], [283])),
+    ("cl", 3, 1, ([312], [273])),
+    ("mp", 3, 1, ([313], [289])),
+    ("fo", 1, 0, 0, ([342, 338, 315], [342, 322, 363])),
+    ("mp", 3, 2, ([319], [269])),
+    ("meet", 3, ([320], [291])),
+    ("fo", 1, 1, 0, ([334, 341, 326], [335, 308, 327])),
+    ("yo", 1, 0, ([328], [319])),
+    ("yo", 1, 1, ([329], [309])),
+    ("m2", 3, ([330], [297])),
+    ("fo", 1, 0, 1, ([387, 333, 331], [340, 323, 251])),
+    ("ca", 0, 3, ([332], [302])),
+    ("ca", 2, 3, ([335], [278])),
+    ("m3", 3, ([337], [305])),
+    ("fo", 1, 1, 1, ([340, 343, 339], [344, 330, 294])),
+    ("sh", 3, ([344], [312])),
+    ("ap", 3, 0, ([345], [313])),
+    ("ys", 3, 0, ([362, 359, 346], [320, 314, 372])),
+    ("ap", 3, 2, ([347], [317])),
+    ("fo", 3, 2, 1, ([356, 355, 348], [348, 337, 395])),
+    ("fo", 3, 3, 1, ([360, 371, 349], [359, 339, 366])),
+    ("fo", 3, 3, 0, ([381, 350, 358], [358, 347, 326])),
+    ("ap", 3, 1, ([351], [333])),
+    ("ys", 3, 1, ([369, 361, 352], [341, 336, 387])),
+    ("fo", 3, 2, 0, ([383, 354, 353], [365, 349, 334])),
+    ("fo", 3, 0, 1, ([379, 374, 357], [362, 352, 381])),
+    ("fo", 3, 0, 0, ([382, 372, 363], [361, 351, 377])),
+    ("fo", 3, 1, 0, ([386, 378, 364], [369, 355, 385])),
+    ("co", 0, 1, ([366], [375])),
+    ("co", 2, 1, ([367], [367])),
+    ("fo", 3, 1, 1, ([390, 376, 368], [370, 356, 350])),
+    ("ca", 1, 3, ([370], [343])),
+    ("yo", 3, 0, ([373], [321])),
+    ("co", 2, 2, ([375], [346])),
+    ("yo", 3, 1, ([377], [364])),
+    ("co", 1, 0, ([380], [378])),
+    ("co", 0, 0, ([384], [357])),
+    ("co", 0, 2, ([385], [353])),
+    ("co", 1, 1, ([388], [360])),
+    ("co", 2, 0, ([389], [354])),
+    ("ca", 3, 3, ([391], [371])),
+    ("co", 3, 0, ([392], [379])),
+    ("co", 1, 2, ([393], [373])),
+    ("co", 3, 1, ([394], [383])),
+    ("co", 3, 2, ([395], [380])),
 ]
 
 
@@ -369,7 +369,7 @@
     across = device(1 - y, z, core)
     toward = (device(y, z + 1, core), device(y, z - 1, core))
     can = (z < length - 1, z > 0)
-    edge = (z == 0, z == length - 1)
+    at_end = (z == 0) | (z == length - 1)
     partners = [(atom, lax.rem(band + k, bands)) for k in range(1, bands)]
 
     def span(side, start, size):
@@ -426,16 +426,15 @@
     def cols(chunk):
         return pl.ds(chunk[0], chunk[1])
 
-    def a_z(g, f, block, d, own=False):
+    def a_z(g, f, block, d):
         c, lane = gather_flows[g][f]
         piece = gath.at[g, lane, block, :, cols(gather_plan[g][c])]
-        sent = length if own and d else block
-        return remote(piece, piece, az_s.at[g, f, sent], az_r.at[g, f, block], toward[d])
+        return remote(piece, piece, az_s.at[g, f], az_r.at[g, f, block], toward[d])
 
     def a_y(g, c, block):
         where = cols(gather_plan[g][c])
         return remote(gath.at[g, 0, block, :, where], gath.at[g, 1, block, :, where],
-                      ay_s.at[g, c, block], ay_r.at[g, c, block], across)
+                      ay_s.at[g, c], ay_r.at[g, c], across)
 
     def start_across(g, c):
         a_y(g, c, z).start()
@@ -443,7 +442,7 @@
     def start_along(g, f, d):
         @pl.when(can[d])
         def _():
-            a_z(g, f, z, d, True).start()
+            a_z(g, f, z, d).start()
 
     def enter(g, c):
         a_y(g, c, z).wait_recv()
@@ -469,15 +468,18 @@
             a_y(g, c, block).start()
 
     def gather_close(g, c):
-        for block in range(length):
-            a_y(g, c, block).wait_recv()
+        piece = gath.at[g, 1, :, :, cols(gather_plan[g][c])]
+        remote(piece, piece, ay_s.at[g, c], ay_r.at[g, c], across).wait_recv()
+
+    def widest(size):
+        return next(unit * n for n in (8, 7, 5, 4, 3, 2, 1) if size % (unit * n) == 0)
 
     keep, give = core, other
     met = set()
 
     def meet(g, c):
         start, size, _ = gather_plan[g][c]
-        kt = next(unit * n for n in (2, 1) if size % (unit * n) == 0)
+        kt = widest(size)
 
         def body(t, acc):
             where = pl.ds(pl.multiple_of(start + t * kt, unit), kt)
@@ -532,21 +534,22 @@
     def r_y(g, c, block):
         where = cols(scatter_plan[g][c])
         return remote(ysend.at[g, block, :, where], yrecv.at[g, block, :, where],
-                      ry_s.at[g, c, block], ry_r.at[g, c, block], across)
+                      ry_s.at[g, c], ry_r.at[g, c, block], across)
 
     def r_z(g, f, block, d, last):
         c, lane = scatter_flows[g][f]
         where = cols(scatter_plan[g][c])
         lands = length if last and d else block
         return remote(slot.at[g, lane, block, :, where], slot.at[g, lane, lands, :, where],
-                      rz_s.at[g, f, block], rz_r.at[g, f, lands], toward[d])
+                      rz_s.at[g, f], rz_r.at[g, f, lands], toward[d])
 
     def tiles(chunk, body):
         start, size, _ = chunk
-
-        @pl.loop(0, size // unit)
+        wide = widest(size)
+
+        @pl.loop(0, size // wide)
         def _(t):
-            body(pl.ds(pl.multiple_of(start + t * unit, unit), unit))
+            body(pl.ds(pl.multiple_of(start + t * wide, unit), wide))
 
     def apply(g, c):
         chunk = scatter_plan[g][c]
@@ -555,11 +558,11 @@
             new = jnp.dot(weights[g].reshape(2 * half_rows, both), full[:, where],
                           preferred_element_type=jnp.float32)
             if chunk[2]:
-                term[g, 0, :, :, where] = new[:half_rows].reshape(length, rows, unit)
-                ysend[g, :, :, where] = new[half_rows:].reshape(length, rows, unit).astype(
+                term[g, 0, :, :, where] = new[:half_rows].reshape(length, rows, -1)
+                ysend[g, :, :, where] = new[half_rows:].reshape(length, rows, -1).astype(
                     ysend.dtype)
             else:
-                term[g, :, :, :, where] = new.reshape(2, length, rows, unit)
+                term[g, :, :, :, where] = new.reshape(2, length, rows, -1)
 
         tiles(chunk, body)
 
@@ -686,11 +689,44 @@
         mixes[core] = mix_matrix(table, index, count)
         mix_out.start()
 
+    def sent(piece, sem):
+        remote(piece, piece, sem, sem, peer).wait_send()
+
+    def gather_sent():
+        for g in range(groups):
+            for c, chunk in enumerate(gather_plan[g]):
+                blocks = slice(None) if chunk[2] else pl.ds(z, 1)
+                sent(gath.at[g, 0, blocks, :, cols(chunk)], ay_s.at[g, c])
+            for f, (c, _) in enumerate(gather_flows[g]):
+                where = cols(gather_plan[g][c])
+
+                @pl.when(at_end)
+                def _():
+                    sent(slot.at[g, 0, pl.ds(0, 1), :, where], az_s.at[g, f])
+
+                @pl.when(jnp.logical_not(at_end))
+                def _():
+                    sent(slot.at[g, 0, :, :, where], az_s.at[g, f])
+
+    def scatter_sent(which):
+        for g in which:
+            for c, chunk in enumerate(scatter_plan[g]):
+                blocks = slice(None) if chunk[2] else pl.ds(z, 1)
+                sent(ysend.at[g, blocks, :, cols(chunk)], ry_s.at[g, c])
+            for f, (c, _) in enumerate(scatter_flows[g]):
+                sent(slot.at[g, 0, pl.ds(0, length - 1), :, cols(scatter_plan[g][c])],
+                     rz_s.at[g, f])
+
     def play(steps):
         met.clear()
         prepared = ready = False
         inside = set()
-        for name, *rest in steps:
+        last = steps.index(next(s for s in steps if s[:2] == ("co", groups - 1)))
+        for at, (name, *rest) in enumerate(steps):
+            if at == last:
+                gather_sent()
+            if at == len(steps) - 1:
+                scatter_sent(range(groups - 1))
             if name in ("ay", "az") and rest[0] not in inside:
                 entered(rest[0])
                 inside.add(rest[0])
@@ -704,8 +740,6 @@
                 ready = True
             run[name](*rest)
 
-    at_end = edge[0] | edge[1]
-
     @pl.when(at_end)
     def _():
         play(steps[0])
@@ -714,46 +748,14 @@
     def _():
         play(steps[1])
 
+    scatter_sent([groups - 1])
     for c in own_out:
         c.wait_send()
     proj_out.wait_send()
     mix_out.wait_send()
     for g in range(groups):
         share(g, keep).wait_send()
-        for f, (c, lane) in enumerate(gather_flows[g]):
-            @pl.loop(0, length)
-            def _(block):
-                @pl.when((block <= z) & can[0])
-                def _():
-                    a_z(g, f, block, 0).wait_send()
-
-                @pl.when((block > z) & can[1])
-                def _():
-                    a_z(g, f, block, 1).wait_send()
-
-            @pl.when(can[1])
-            def _():
-                a_z(g, f, z, 1, True).wait_send()
-        for f in range(len(scatter_flows[g])):
-            @pl.loop(0, length)
-            def _(block):
-                @pl.when(block != z)
-                def _():
-                    r_z(g, f, block, 0, False).wait_send()
-        for c, chunk in enumerate(gather_plan[g]):
-            if chunk[2]:
-                @pl.loop(0, length)
-                def _(block):
-                    a_y(g, c, block).wait_send()
-            else:
-                a_y(g, c, z).wait_send()
-        for c, chunk in enumerate(scatter_plan[g]):
-            if chunk[2]:
-                @pl.loop(0, length)
-                def _(block):
-                    r_y(g, c, block).wait_send()
-            else:
-                r_y(g, c, z).wait_send()
+        for c in range(len(scatter_plan[g])):
             local, far, coming = result(g, c)
 
             @pl.when(core == g % 2)
@@ -803,10 +805,10 @@
             pltpu.VMEM(dij_table.shape[1:] + dij_table.shape[:1], f32),
             pltpu.SMEM(dij_index.shape, jnp.int32), pltpu.SMEM(proj_count.shape, jnp.int32),
             dma((3,)), dma((groups // 2 + 1,)), dma((2, groups // 2)), dma((2,)), dma((2,)),
-            dma((groups, flows, length + 1)), dma((groups, flows, length)),
-            dma((groups, chunks, length)), dma((groups, chunks, length)),
-            dma((groups, flows, length)), dma((groups, flows, length + 1)),
-            dma((groups, chunks, length)), dma((groups, chunks, length)),
+            dma((groups, flows)), dma((groups, flows, length)),
+            dma((groups, chunks)), dma((groups, chunks)),
+            dma((groups, flows)), dma((groups, flows, length + 1)),
+            dma((groups, chunks)), dma((groups, chunks, length)),
             dma((2, groups)), dma((groups, others)), dma((groups, others)), dma((2, groups)),
             dma((2, groups, chunks)), dma((groups, chunks)),
         ],

time: 147 us -> 143 us (0.973)
  Pallas kernels: 145 us -> 140 us
    pallas_call x1, Pallas kernels: 145 us -> 140 us  [shards(): pl.pallas_call(functools.partial(kernel, length, bands, gather_plan, scat...]
where the time goes in v4:
time: 143 us
  Pallas kernels  140 us (98%)
  local copies, waits for them, and re-layouts  2.26 us (2%)
    pallas_call x1, Pallas kernels, shards(): pl.pallas_call(functools.partial(kernel, length, bands, gather_plan, scat...  140 us

profile of v4, /device:TPU:0, one launch (start us, length us, event | category | flops | bytes accessed | tf_op | source)
XLA Modules:
  0.0 142.6 jit_solution(14768632165143958281)
XLA Ops:
  0.0 140.3 %shard_map.68 = bf16[16,32768]{1,0:T(8,128)(2,1)} custom-call(bf16[16,32768]{1,0:T(8,128)(2,1)} %wave.1, bf16[128,32768]{1,0:T(8,128)(2,1)} %proj.1, f32[8,8,16]{2,1,0:T(8,128)} %bitcast.1, s32[16]{0:T(128)} %index_in.1, s32[16]{0:T(128)} %count_in.1), custom_call_target="tpu_custom_call" | custom-call | tf_op jit(solution)/jit(shards)/shard_map/pallas_call | solution.py:788
  140.3 2.3 %copy.7 = bf16[16,32768]{1,0:T(8,128)(2,1)} copy(bf16[16,32768]{1,0:T(8,128)(2,1)} %shard_map.68) | data formatting | bytes 2097152
